TPU v7x, 32 devices: a whole 2x2x4 slice. The times are simulated.
32 devices in a mesh: gx: 2 (over core), gyz: 16 (over z, y, x).
Axes of the slice: x: 2, y: 2, z: 4, core: 2. Of those that a mesh axis runs over, the one named last changes fastest.
Arguments:
- bands: bfloat16 [16, 80, 40, 512], P('gx', 'gyz'), may hold values from -6 to 6
- potential: float32 [16, 80, 40], P('gx', 'gyz'), may hold values from 0.5 to 4
- eigenvectors: bfloat16 [512, 512], P('gyz'), may hold values from -0.25 to 0.25
Outputs:
- correlation: float32 [512, 512], P('gyz')
- hamiltonian: float32 [512, 512], P('gyz')
- rotated: bfloat16 [16, 80, 40, 512], P('gx', 'gyz')
All inputs are finite; a program needn't handle non-finite values.
Results may differ from a plain program's by a relative error of at most 0.0012.
Values may be sent and summed in bfloat16 or wider, within the bound.
A program may use at most 64 MiB of HBM per device.

v0:
```python
import functools
import itertools

import jax
import jax.numpy as jnp
from jax import lax
from jax.experimental import pallas as pl
from jax.experimental.pallas import tpu as pltpu
from jax.sharding import PartitionSpec as P

MESH = pl.DeviceIdType.MESH
F32 = jnp.float32


def digit_sizes(count):
    sizes = []
    while count > 1:
        size = 4 if count % 4 == 0 else (2 if count % 2 == 0 else count)
        sizes.append(size)
        count //= size
    return tuple(reversed(sizes)) or (1,)


def gram_t(left, right):
    return lax.dot_general(left, right, (((0,), (0,)), ((), ())), preferred_element_type=F32)


class Copies:
    def __init__(self, send_sems, recv_sems):
        self.send_sems, self.recv_sems, self.used = send_sems, recv_sems, 0

    def make(self, src, dst, device_id):
        slot = self.used
        self.used += 1
        return pltpu.make_async_remote_copy(
            src_ref=src, dst_ref=dst, send_sem=self.send_sems.at[slot],
            recv_sem=self.recv_sems.at[slot], device_id=device_id, device_id_type=MESH)


def streams_of(rows, count):
    fast, slow = tuple(range(count))[::-1], tuple(range(count))
    if rows % 32 or count == 1:
        return ((0, rows, fast),), ((0, rows, fast),)
    plans = []
    for parts in (H_PARTS, C_PARTS):
        cut = rows // 4 * parts
        plans.append(tuple(p for p in ((0, cut, fast), (cut, rows, slow)) if p[1] > p[0]))
    return tuple(plans)


H_PARTS, C_PARTS = 4, 2


class Stream:
    def __init__(self, context, source, first, last, order, received, parts):
        self.context, self.source, self.order = context, source, order
        self.rows, self.received, self.parts = slice(first, last), received, parts
        self.left, self.phase = list(range(len(order))), 0

    def index(self, value):
        d = self.order[self.phase]
        at = tuple(value if i == d else slice(None) for i in self.left)
        return at + (self.rows,) if self.phase == 0 else at

    def start(self):
        copies, sizes, digits, gx, peer = self.context
        d = self.order[self.phase]
        self.flying = []
        for k in range(1, sizes[d]):
            target, digit = peer(d, k)
            copy = copies.make(self.source.at[self.index(digit)],
                               self.received[self.phase].at[k - 1], (gx, target))
            copy.start()
            self.flying.append(copy)

    def finish(self):
        copies, sizes, digits, gx, peer = self.context
        d = self.order[self.phase]
        for copy in self.flying:
            copy.wait_recv()
        total = self.source[self.index(digits[d])]
        for k in range(1, sizes[d]):
            total = total + self.received[self.phase][k - 1]
        self.parts[self.phase][...] = total
        self.source = self.parts[self.phase]
        self.left.remove(d)
        self.phase += 1


def kernel(geometry, grid4, rows_in, pot_in, eig, corr_out, ham_out, rot_out, flat, pot, coef, padded, hq,
           corr, ham, halo_y, halo_x, pair_c, pair_h, sum_c, sum_h, gx_c, gx_h,
           send_sems, recv_sems, local_sems, *buffers):
    gx_size, gyz_size, cx, cy, cz, bands, rows, sizes, copy_count = geometry
    count = len(sizes)
    half = bands // 2
    gx, gyz = lax.axis_index("gx"), lax.axis_index("gyz")
    parity = lax.rem(gx, 2)
    partner = gx + 1 - 2 * parity
    mine = pl.ds(pl.multiple_of(parity * half, half), half)
    other = pl.ds(pl.multiple_of((1 - parity) * half, half), half)
    strides = []
    step = gyz_size
    for size in sizes:
        step //= size
        strides.append(step)
    digits = [lax.rem(gyz // stride, size) for stride, size in zip(strides, sizes)]
    copies = Copies(send_sems, recv_sems)

    def peer(d, k):
        digit = lax.rem(digits[d] + k, sizes[d])
        return gyz + (digit - digits[d]) * strides[d], digit

    load_flat = pltpu.make_async_copy(rows_in, flat, local_sems.at[0])
    load_flat.start()
    own_coef = coef.at[tuple(digits) + (slice(None), mine)]
    load_coef = pltpu.make_async_copy(eig.at[:, mine], own_coef, local_sems.at[1])
    load_coef.start()
    load_pot = pltpu.make_async_copy(pot_in, pot, local_sems.at[2])
    load_pot.start()

    barrier = pltpu.get_barrier_semaphore()
    greeted = [(gx, lax.rem(gyz + 1, gyz_size)), (gx, lax.rem(gyz + gyz_size - 1, gyz_size)),
               (lax.rem(gx + 1, gx_size), gyz), (lax.rem(gx + gx_size - 1, gx_size), gyz),
               (partner, gyz)]
    for d, size in enumerate(sizes):
        greeted += [(gx, peer(d, k)[0]) for k in range(1, size)]
    greeted += [(lax.rem(gx + 2 * k, gx_size), gyz) for k in range(1, gx_size // 2)]
    for device in greeted:
        pl.semaphore_signal(barrier, inc=1, device_id=device, device_id_type=MESH)
    pl.semaphore_wait(barrier, len(greeted))

    sent = []

    def coef_phase(d):
        started = []
        for k in range(1, sizes[d]):
            index = tuple(digits[:d + 1] + [slice(None)] * (count - 1 - d)) + (slice(None), mine)
            block = coef.at[index]
            copy = copies.make(block, block, (gx, peer(d, k)[0]))
            copy.start()
            started.append(copy)
        sent.extend(started)
        return started

    def next_coef_phase(started, d):
        for copy in started:
            copy.wait_recv()
        return coef_phase(count - 1 - d) if d < count else []

    load_coef.wait()
    coef_copies = coef_phase(count - 1)

    to_x = copies.make(grid4.at[cx - 1], halo_x, (lax.rem(gx + 1, gx_size), gyz))
    to_y = copies.make(grid4.at[:, cy - 1], halo_y, (gx, lax.rem(gyz + 1, gyz_size)))
    last_x, last_y = gx == gx_size - 1, gyz == gyz_size - 1

    @pl.when(jnp.logical_not(last_y))
    def _():
        to_y.start()

    @pl.when(jnp.logical_not(last_x))
    def _():
        to_x.start()

    @pl.when(gx == 0)
    def _():
        halo_x[...] = jnp.zeros_like(halo_x)

    @pl.when(gyz == 0)
    def _():
        halo_y[...] = jnp.zeros_like(halo_y)

    def block_index(block):
        index = []
        for stride in strides:
            index.append(block // stride)
            block %= stride
        return tuple(index)

    def store_rows(target, first, value):
        for j in range(value.shape[0] // rows):
            target[block_index(first // rows + j)] = value[j * rows:(j + 1) * rows]

    tile = min(bands, 256)
    load_flat.wait()
    for first in range(0, bands, tile):
        store_rows(corr, first, gram_t(flat[:, first:first + tile], flat[...]))
    everything = tuple([slice(None)] * (count + 1))
    pair_copy_c = copies.make(corr.at[everything + (other,)], pair_c, (partner, gyz))
    pair_copy_c.start()
    load_pot.wait()

    plane = cy * cz
    cells = cx * plane
    chunk = 2 * cz if cells % (2 * cz) == 0 else cz
    for first in range(0, cells, chunk):
        padded[first:first + chunk] = flat[first:first + chunk].astype(F32)
    row = lax.broadcasted_iota(jnp.int32, (cz, cz), 0)
    column = lax.broadcasted_iota(jnp.int32, (cz, cz), 1)
    zero_row = jnp.zeros((1, bands), F32)

    def segment(x, y):
        at = x * plane + y * cz
        centre = padded[at:at + cz]
        near = jnp.concatenate([zero_row, centre[:-1]]) + jnp.concatenate([centre[1:], zero_row])
        for there, offset in ((x > 0, -plane), (x < cx - 1, plane), (y > 0, -cz), (y < cy - 1, cz)):
            if there:
                near = near + padded[at + offset:at + offset + cz]
        local = jnp.broadcast_to(pot[y, x:x + 1, :], (cz, cz))
        factor = 3.0 + jnp.sum(jnp.where(row == column, local, 0.0), axis=1, keepdims=True)
        return factor * centre - 0.5 * near

    order = list(itertools.product(range(cx), range(cy)))
    per = chunk // cz
    for first in range(0, len(order), per):
        hq[first * cz:(first + per) * cz] = jnp.concatenate(
            [segment(*xy) for xy in order[first:first + per]]).astype(jnp.bfloat16)

    context = (copies, sizes, digits, gx, peer)
    ham_plan, corr_plan = streams_of(rows, count)
    taken = iter(buffers)

    def streams(plan, source):
        made = []
        for first, last, digit_order in plan:
            received = [next(taken) for _ in digit_order]
            parts = [next(taken) for _ in digit_order]
            made.append(Stream(context, source, first, last, digit_order, received, parts))
        return made

    ham_streams, corr_streams = streams(ham_plan, sum_h), streams(corr_plan, sum_c)

    def begin(group):
        for stream in group:
            stream.start()

    def end(group):
        for stream in group:
            stream.finish()
            sent.extend(stream.flying)
            if stream.phase < count:
                stream.start()

    pair_copy_c.wait_recv()
    sum_c[...] = corr[everything + (mine,)] + pair_c[...]
    begin(corr_streams)
    coef_copies = next_coef_phase(coef_copies, 1)

    for first in range(0, bands, tile):
        store_rows(ham, first, gram_t(flat[:, first:first + tile], hq[...]))

    @pl.when(gyz > 0)
    def _():
        to_y.wait_recv()

    @pl.when(gx > 0)
    def _():
        to_x.wait_recv()

    first_y = jnp.concatenate([flat[x * plane:x * plane + cz] for x in range(cx)])
    ghost_y = jnp.concatenate([halo_y[x] for x in range(cx)])
    first_x = flat[0:plane]
    ghost_x = jnp.concatenate([halo_x[y] for y in range(cy)])
    cross = padded.at[0:bands]
    for first in range(0, bands, tile):
        cut = slice(first, first + tile)
        cross[cut] = -0.5 * (gram_t(first_y[:, cut], ghost_y) + gram_t(first_x[:, cut], ghost_x))
    for first in range(0, bands, tile):
        cut = slice(first, first + tile)
        value = cross[cut] + jnp.transpose(cross[:, cut])
        for j in range(tile // rows):
            index = block_index(first // rows + j)
            ham[index] = ham[index] + value[j * rows:(j + 1) * rows]
    pair_copy_h = copies.make(ham.at[everything + (other,)], pair_h, (partner, gyz))
    pair_copy_h.start()
    pair_copy_h.wait_recv()
    sum_h[...] = ham[everything + (mine,)] + pair_h[...]
    begin(ham_streams)

    for d in range(2, count + 1):
        coef_copies = next_coef_phase(coef_copies, d)
    mine_block = coef.at[everything + (mine,)]
    pair_copy_e = copies.make(mine_block, mine_block, (partner, gyz))
    pair_copy_e.start()

    scale = 1.0 / (cells * gyz_size)

    def last_sum(group, gx_recv, final):
        for at, stream in enumerate(group):
            final[stream.rows, mine] = stream.source[...]
        others = []
        for k in range(1, gx_size // 2):
            target = (lax.rem(gx + 2 * k, gx_size), gyz)
            copy = copies.make(final.at[:, mine], gx_recv.at[k - 1], target)
            copy.start()
            others.append(copy)
        for copy in others:
            copy.wait()
        total = final[:, mine]
        for k in range(1, gx_size // 2):
            total = total + gx_recv[k - 1]
        final[:, mine] = total * scale
        copy = copies.make(final.at[:, mine], final.at[:, mine], (partner, gyz))
        copy.start()
        return copy

    end(corr_streams)
    end(ham_streams)
    pair_copy_e.wait_recv()
    whole = coef[...].reshape(bands, bands)
    part = max(size for size in range(16, 512, 16) if cells % size == 0)
    for first in range(0, cells, part):
        rot_out[first:first + part] = jnp.dot(
            flat[first:first + part], whole, preferred_element_type=F32).astype(jnp.bfloat16)

    for _ in range(count - 1):
        end(corr_streams)
    last_c = last_sum(corr_streams, gx_c, corr_out)
    for _ in range(count - 1):
        end(ham_streams)
    last_h = last_sum(ham_streams, gx_h, ham_out)

    last_c.wait_recv()
    last_h.wait_recv()
    for copy in sent + [pair_copy_c, pair_copy_h, pair_copy_e, last_c, last_h]:
        copy.wait_send()

    @pl.when(jnp.logical_not(last_y))
    def _():
        to_y.wait_send()

    @pl.when(jnp.logical_not(last_x))
    def _():
        to_x.wait_send()

    assert copies.used == copy_count


def deliver(corr, ham, rot, corr_out, ham_out, rot_out, sems):
    copies = [pltpu.make_async_copy(source, target, sems.at[i]) for i, (source, target) in
              enumerate(((rot, rot_out), (corr, corr_out), (ham, ham_out)))]
    for copy in copies:
        copy.start()
    for copy in copies:
        copy.wait()


def in_hbm(array):
    return pltpu.with_memory_space_constraint(array, pltpu.HBM)


def on_device(bands, potential, eigenvectors):
    gx_size, gyz_size = lax.axis_size("gx"), lax.axis_size("gyz")
    cx, cy, cz, width = bands.shape
    rows = eigenvectors.shape[0]
    cells = cx * cy * cz
    sizes = digit_sizes(gyz_size)
    count = len(sizes)
    half = width // 2
    flat = bands.reshape(cells, width)
    ham_plan, corr_plan = streams_of(rows, count)
    per_stream = sum(s - 1 for s in sizes)
    copy_count = 2 + (1 + len(ham_plan) + len(corr_plan)) * per_stream + 3 + 2 * (gx_size // 2)
    geometry = (gx_size, gyz_size, cx, cy, cz, width, rows, sizes, copy_count)

    buffers = []
    for first, last, order in ham_plan + corr_plan:
        received, parts, left = [], [], list(range(count))
        for d in order:
            left.remove(d)
            shape = tuple(sizes[i] for i in left) + (last - first, half)
            received.append(pltpu.VMEM((sizes[d] - 1,) + shape, F32))
            parts.append(pltpu.VMEM(shape, F32))
        buffers += received + parts

    wide, narrow = sizes + (rows, width), sizes + (rows, half)
    others = max(gx_size // 2 - 1, 1)
    vmem, anywhere = pl.BlockSpec(memory_space=pltpu.VMEM), pl.BlockSpec(memory_space=pl.ANY)
    results = (jax.ShapeDtypeStruct((rows, width), F32), jax.ShapeDtypeStruct((rows, width), F32),
               jax.ShapeDtypeStruct((cells, width), jnp.bfloat16))
    computed = pl.pallas_call(
        functools.partial(kernel, geometry),
        out_shape=results,
        in_specs=[pl.BlockSpec(memory_space=pltpu.HBM)] * 4,
        out_specs=(vmem, vmem, vmem),
        scratch_shapes=[
            pltpu.VMEM((cells, width), jnp.bfloat16), pltpu.VMEM((cy, cx, cz), F32),
            pltpu.VMEM(wide, jnp.bfloat16),
            pltpu.VMEM((cells, width), F32), pltpu.VMEM((cells, width), jnp.bfloat16),
            pltpu.VMEM(wide, F32), pltpu.VMEM(wide, F32),
            pltpu.VMEM((cx, cz, width), jnp.bfloat16), pltpu.VMEM((cy, cz, width), jnp.bfloat16),
            pltpu.VMEM(narrow, F32), pltpu.VMEM(narrow, F32),
            pltpu.VMEM(narrow, F32), pltpu.VMEM(narrow, F32),
            pltpu.VMEM((others, rows, half), F32), pltpu.VMEM((others, rows, half), F32),
            pltpu.SemaphoreType.DMA((copy_count,)), pltpu.SemaphoreType.DMA((copy_count,)),
            pltpu.SemaphoreType.DMA((3,)), *buffers,
        ],
        compiler_params=pltpu.CompilerParams(
            collective_id=0, has_side_effects=True, vmem_limit_bytes=52 * 1024 * 1024),
    )(bands, flat, in_hbm(jnp.transpose(potential, (1, 0, 2))), in_hbm(eigenvectors))
    corr, ham, rotated = pl.pallas_call(
        deliver, out_shape=results, in_specs=[vmem] * 3, out_specs=[anywhere] * 3,
        scratch_shapes=[pltpu.SemaphoreType.DMA((3,))],
        compiler_params=pltpu.CompilerParams(vmem_limit_bytes=8 * 1024 * 1024),
    )(*computed)
    return corr, ham, rotated.reshape(bands.shape)


def solution(mesh):
    in_specs = (P("gx", "gyz", None, None), P("gx", "gyz", None), P("gyz", None))
    out_specs = (P("gyz", None), P("gyz", None), P("gx", "gyz", None, None))
    return jax.shard_map(
        on_device, mesh=mesh, in_specs=in_specs, out_specs=out_specs, check_vma=False
    )
```

profile of v0, /device:TPU:0, one launch (start us, length us, event | category | flops | bytes accessed | tf_op | source)
XLA Modules:
  0.0 32.6 jit_solution(16364790490611537705)
XLA Ops:
  0.6 30.8 %shard_map.58 = (f32[32,512]{1,0:T(8,128)S(1)}, f32[32,512]{1,0:T(8,128)S(1)}, bf16[1600,512]{1,0:T(8,128)(2,1)S(1)}) custom-call(bf16[8,5,40,512]{3,2,1,0:T(8,128)(2,1)} %grid4.1, bf16[1600,512]{1,0:T(8,128)(2,1)} %bitcast.3, f32[5,8,40]{2,1,0:T(8,128)} %bitcast.4, bf16[32,512]{1,0:T(8,128)(2,1)} %eig.1), custom_call_target="tpu_custom_call" | custom-call | tf_op jit(solution)/shard_map/pallas_call | solution.py:381
  31.4 1.2 %shard_map.59 = (f32[32,512]{1,0:T(8,128)}, f32[32,512]{1,0:T(8,128)}, bf16[1600,512]{1,0:T(8,128)(2,1)}) custom-call(f32[32,512]{1,0:T(8,128)S(1)} %get-tuple-element.9.corr, f32[32,512]{1,0:T(8,128)S(1)} %get-tuple-element.10.ham, bf16[1600,512]{1,0:T(8,128)(2,1)S(1)} %get-tuple-element.11.rot), custom_call_target="tpu_custom_call" | custom-call | tf_op jit(solution)/shard_map/pallas_call | solution.py:401
where the time goes:
time: 33.1 us; the launch traced here: 32.6 us
  Pallas kernels  32 us (97%)
  between operations  0.64 us (2%)
    pallas_call x1, Pallas kernels, on_device(): pl.pallas_call(functools.partial(kernel, geometry), out_shape=results, in...  30.8 us
    pallas_call x1, Pallas kernels, on_device(): pl.pallas_call(deliver, out_shape=results, in_specs=[vmem] * 3, out_specs...  1.22 us

commit v1 on v0

v1 whole, which is shorter than its diff:
```python
import functools
import itertools
import math

import jax
import jax.numpy as jnp
from jax import lax
from jax.experimental import pallas as pl
from jax.experimental.pallas import tpu as pltpu
from jax.sharding import PartitionSpec as P

MESH = pl.DeviceIdType.MESH
F32, BF16 = jnp.float32, jnp.bfloat16
scope = jax.named_scope


def digit_sizes(count):
    sizes, base = [], 2 if count <= 16 else 4
    while count > 1:
        size = base if count % base == 0 else (2 if count % 2 == 0 else count)
        sizes.append(size)
        count //= size
    return tuple(reversed(sizes)) or (1,)


def gram_t(left, right):
    return lax.dot_general(left, right, (((0,), (0,)), ((), ())), preferred_element_type=F32)


class Copies:
    def __init__(self, send_sems, recv_sems):
        self.send_sems, self.recv_sems, self.used = send_sems, recv_sems, 0

    def make(self, src, dst, device_id):
        slot = self.used
        self.used += 1
        return pltpu.make_async_remote_copy(
            src_ref=src, dst_ref=dst, send_sem=self.send_sems.at[slot],
            recv_sem=self.recv_sems.at[slot], device_id=device_id, device_id_type=MESH)


def singles(order):
    return tuple((d,) for d in order)


def plans_of(rows, sizes):
    count = len(sizes)
    if sizes == (2, 2, 2, 2) and rows % 32 == 0:
        ham = ((0, rows // 2, ((2, 3), (0, 1))), (rows // 2, rows, ((0, 1), (2, 3))))
        corr = ((0, rows, ((0, 1), (2, 3))),)
        return ham, corr, ((0, 1), (3,), (2,))
    fast, slow = singles(range(count)[::-1]), singles(range(count))
    return ((0, rows, fast),), ((0, rows, slow),), slow


def peer_count(sizes, group):
    return math.prod(sizes[d] for d in group)


def copies_of(sizes, order):
    return sum(peer_count(sizes, group) - 1 for group in order)


class Stream:
    def __init__(self, context, source, first, last, order, outgoing, received, parts):
        self.context, self.source, self.order, self.outgoing = context, source, order, outgoing
        self.rows, self.received, self.parts = slice(first, last), received, parts
        self.left, self.phase = list(range(len(context[1]))), 0

    def index(self, values):
        at = tuple(values[d] if d in values else slice(None) for d in self.left)
        return at

    def current(self):
        everything = tuple(slice(None) for _ in self.left)
        return self.source[everything + (self.rows,)] if self.phase == 0 else self.source[...]

    def start(self):
        copies, sizes, digits, gx, peer = self.context
        group = self.order[self.phase]
        self.flying = []
        out = self.outgoing[self.phase]
        out[...] = self.current().astype(BF16)
        for k in range(1, peer_count(sizes, group)):
            target, values = peer(group, k)
            copy = copies.make(out.at[self.index(values)],
                               self.received[self.phase].at[k - 1], (gx, target))
            copy.start()
            self.flying.append(copy)

    def finish(self):
        copies, sizes, digits, gx, peer = self.context
        group = self.order[self.phase]
        for copy in self.flying:
            copy.wait_recv()
        own = self.index({d: digits[d] for d in group})
        total = self.source[own + (self.rows,) if self.phase == 0 else own]
        for k in range(1, peer_count(sizes, group)):
            total = total + self.received[self.phase][k - 1].astype(F32)
        self.parts[self.phase][...] = total
        self.source = self.parts[self.phase]
        self.left = [d for d in self.left if d not in group]
        self.phase += 1


def kernel(geometry, grid4, rows_in, pot_in, eig, corr_out, ham_out, rot_out, flat, pot, coef, padded, hq,
           corr, ham, halo_f, halo_b, halo_x, own, ghost, pair_c, pair_h, sum_c, sum_h, gx_c, gx_h,
           send_sems, recv_sems, local_sems, *buffers):
    gx_size, gyz_size, cx, cy, cz, bands, rows, sizes, copy_count = geometry
    ham_plan, corr_plan, coef_plan = plans_of(rows, sizes)
    count = len(sizes)
    half = bands // 2
    gx, gyz = lax.axis_index("gx"), lax.axis_index("gyz")
    parity = lax.rem(gx, 2)
    partner = gx + 1 - 2 * parity
    mine = pl.ds(pl.multiple_of(parity * half, half), half)
    other = pl.ds(pl.multiple_of((1 - parity) * half, half), half)
    strides = []
    step = gyz_size
    for size in sizes:
        step //= size
        strides.append(step)
    digits = [lax.rem(gyz // stride, size) for stride, size in zip(strides, sizes)]
    copies = Copies(send_sems, recv_sems)

    def peer(group, k):
        target, values = gyz, {}
        for d in reversed(group):
            digit = lax.rem(digits[d] + k % sizes[d], sizes[d])
            target = target + (digit - digits[d]) * strides[d]
            values[d] = digit
            k //= sizes[d]
        return target, values

    load_flat = pltpu.make_async_copy(rows_in, flat, local_sems.at[0])
    load_flat.start()
    own_coef = coef.at[tuple(digits) + (slice(None), mine)]
    load_coef = pltpu.make_async_copy(eig.at[:, mine], own_coef, local_sems.at[1])
    load_coef.start()
    load_pot = pltpu.make_async_copy(pot_in, pot, local_sems.at[2])
    load_pot.start()

    barrier = pltpu.get_barrier_semaphore()
    first_x, last_x, first_y, last_y = gx == 0, gx == gx_size - 1, gyz == 0, gyz == gyz_size - 1
    beside = ((first_x, (gx - 1, gyz)), (last_x, (gx + 1, gyz)), (first_y, (gx, gyz - 1)), (last_y, (gx, gyz + 1)))
    for edge, device in beside:
        @pl.when(jnp.logical_not(edge))
        def _():
            pl.semaphore_signal(barrier, inc=1, device_id=device, device_id_type=MESH)
    neighbours = sum(1 - edge.astype(jnp.int32) for edge, _ in beside)
    greeted = []
    groups = []
    for _, _, order in ham_plan + corr_plan + ((0, 0, coef_plan),):
        groups += [group for group in order if group not in groups]
    wide = [group for group in groups if not any(set(group) < set(other) for other in groups)]
    for group in wide:
        greeted += [(gx, peer(group, k)[0]) for k in range(1, peer_count(sizes, group))]
    greeted += [(lax.rem(gx + 2 * k, gx_size), gyz) for k in range(1, gx_size // 2)]
    for device in greeted:
        pl.semaphore_signal(barrier, inc=1, device_id=device, device_id_type=MESH)
    with scope("barrier"):
        pl.semaphore_wait(barrier, len(greeted) + neighbours)

    sent = []

    def coef_phase(at):
        started = []
        done = {d for group in coef_plan[:at] for d in group}
        index = tuple(slice(None) if d in done else digits[d] for d in range(count)) + (slice(None), mine)
        for k in range(1, peer_count(sizes, coef_plan[at])):
            block = coef.at[index]
            copy = copies.make(block, block, (gx, peer(coef_plan[at], k)[0]))
            copy.start()
            started.append(copy)
        sent.extend(started)
        return started

    def next_coef_phase(started, at):
        for copy in started:
            copy.wait_recv()
        return coef_phase(at) if at < len(coef_plan) else []


    to_x = copies.make(grid4.at[cx - 1], halo_x, (lax.rem(gx + 1, gx_size), gyz))
    cut_x = (cx + 1) // 2
    ahead = copies.make(grid4.at[:cut_x, cy - 1], halo_f, (gx, lax.rem(gyz + 1, gyz_size)))
    back = copies.make(grid4.at[cut_x:, 0], halo_b, (gx, lax.rem(gyz + gyz_size - 1, gyz_size)))

    @pl.when(jnp.logical_not(last_y))
    def _():
        ahead.start()

    @pl.when(jnp.logical_not(first_y))
    def _():
        back.start()

    @pl.when(jnp.logical_not(last_x))
    def _():
        to_x.start()

    @pl.when(first_x)
    def _():
        halo_x[...] = jnp.zeros_like(halo_x)

    @pl.when(first_y)
    def _():
        halo_f[...] = jnp.zeros_like(halo_f)

    @pl.when(last_y)
    def _():
        halo_b[...] = jnp.zeros_like(halo_b)

    load_coef.wait()
    coef_copies = coef_phase(0)

    def block_index(block):
        index = []
        for stride in strides:
            index.append(block // stride)
            block %= stride
        return tuple(index)

    def store_rows(target, first, value):
        for j in range(value.shape[0] // rows):
            target[block_index(first // rows + j)] = value[j * rows:(j + 1) * rows]

    tile = min(bands, 256)
    with scope('load'):
        load_flat.wait()
    for first in range(0, bands, tile):
        store_rows(corr, first, gram_t(flat[:, first:first + tile], flat[...]))
    everything = tuple([slice(None)] * (count + 1))
    pair_copy_c = copies.make(corr.at[everything + (other,)], pair_c, (partner, gyz))
    pair_copy_c.start()
    load_pot.wait()

    plane = cy * cz
    cells = cx * plane
    chunk = 2 * cz if cells % (2 * cz) == 0 else cz
    for first in range(0, cells, chunk):
        padded[first:first + chunk] = flat[first:first + chunk].astype(F32)
    row = lax.broadcasted_iota(jnp.int32, (cz, cz), 0)
    column = lax.broadcasted_iota(jnp.int32, (cz, cz), 1)
    zero_row = jnp.zeros((1, bands), F32)

    def segment(x, y):
        at = x * plane + y * cz
        centre = padded[at:at + cz]
        near = jnp.concatenate([zero_row, centre[:-1]]) + jnp.concatenate([centre[1:], zero_row])
        for there, offset in ((x > 0, -plane), (x < cx - 1, plane), (y > 0, -cz), (y < cy - 1, cz)):
            if there:
                near = near + padded[at + offset:at + offset + cz]
        local = jnp.broadcast_to(pot[y, x:x + 1, :], (cz, cz))
        factor = 3.0 + jnp.sum(jnp.where(row == column, local, 0.0), axis=1, keepdims=True)
        return factor * centre - 0.5 * near

    order = list(itertools.product(range(cx), range(cy)))
    per = chunk // cz
    for first in range(0, len(order), per):
        hq[first * cz:(first + per) * cz] = jnp.concatenate(
            [segment(*xy) for xy in order[first:first + per]]).astype(BF16)

    context = (copies, sizes, digits, gx, peer)
    taken = iter(buffers)

    def streams(plan, source):
        made = []
        for first, last, digit_order in plan:
            outgoing = [next(taken) for _ in digit_order]
            received = [next(taken) for _ in digit_order]
            parts = [next(taken) for _ in digit_order]
            made.append(Stream(context, source, first, last, digit_order, outgoing, received, parts))
        return made

    ham_streams, corr_streams = streams(ham_plan, sum_h), streams(corr_plan, sum_c)

    def begin(group):
        for stream in group:
            stream.start()

    def end(group):
        for stream in group:
            stream.finish()
            sent.extend(stream.flying)
            if stream.phase < len(stream.order):
                stream.start()

    with scope('pair_c'):
        pair_copy_c.wait_recv()
    sum_c[...] = corr[everything + (mine,)] + pair_c[...]
    begin(corr_streams)

    for first in range(0, bands, tile):
        store_rows(ham, first, gram_t(flat[:, first:first + tile], hq[...]))

    own[...] = jnp.concatenate(
        [flat[x * plane:x * plane + cz] for x in range(cut_x)]
        + [flat[x * plane + plane - cz:x * plane + plane] for x in range(cut_x, cx)] + [flat[0:plane]])

    with scope('halo'):
        @pl.when(jnp.logical_not(first_y))
        def _():
            ahead.wait_recv()

        @pl.when(jnp.logical_not(last_y))
        def _():
            back.wait_recv()

        @pl.when(jnp.logical_not(first_x))
        def _():
            to_x.wait_recv()

    with scope('coef_z'):
        coef_copies = next_coef_phase(coef_copies, 1)

    ghost[...] = jnp.concatenate(
        [halo_f[x] for x in range(cut_x)] + [halo_b[x] for x in range(cx - cut_x)]
        + [halo_x[y] for y in range(cy)])
    cross = padded.at[0:bands]
    for first in range(0, bands, tile):
        cut = slice(first, first + tile)
        cross[cut] = -0.5 * gram_t(own[:, cut], ghost[...])
    for first in range(0, bands, tile):
        cut = slice(first, first + tile)
        value = cross[cut] + jnp.transpose(cross[:, cut])
        for j in range(tile // rows):
            index = block_index(first // rows + j)
            ham[index] = ham[index] + value[j * rows:(j + 1) * rows]
    pair_copy_h = copies.make(ham.at[everything + (other,)], pair_h, (partner, gyz))
    pair_copy_h.start()
    with scope('pair_h'):
        pair_copy_h.wait_recv()
    sum_h[...] = ham[everything + (mine,)] + pair_h[...]
    begin(ham_streams)

    scale = 1.0 / (cells * gyz_size)

    def last_sum(group, gx_recv, final):
        for at, stream in enumerate(group):
            final[stream.rows, mine] = stream.source[...]
        others = []
        for k in range(1, gx_size // 2):
            target = (lax.rem(gx + 2 * k, gx_size), gyz)
            copy = copies.make(final.at[:, mine], gx_recv.at[k - 1], target)
            copy.start()
            others.append(copy)
        for copy in others:
            copy.wait()
        total = final[:, mine]
        for k in range(1, gx_size // 2):
            total = total + gx_recv[k - 1]
        final[:, mine] = total * scale
        copy = copies.make(final.at[:, mine], final.at[:, mine], (partner, gyz))
        copy.start()
        return copy

    coef_steps = len(coef_plan)
    with scope('corr_1'):
        end(corr_streams)
    with scope('coef_x'):
        if coef_steps > 2:
            coef_copies = next_coef_phase(coef_copies, 2)
    with scope('ham_1'):
        end(ham_streams)
    with scope('coef_y'):
        for at in range(min(coef_steps, 3), coef_steps + 1):
            coef_copies = next_coef_phase(coef_copies, at)
    mine_block = coef.at[everything + (mine,)]
    pair_copy_e = copies.make(mine_block, mine_block, (partner, gyz))
    pair_copy_e.start()
    with scope('corr_2'):
        while corr_streams[0].phase < len(corr_plan[0][2]):
            end(corr_streams)
    last_c = last_sum(corr_streams, gx_c, corr_out)
    with scope('pair_e'):
        pair_copy_e.wait_recv()
    whole = coef[...].reshape(bands, bands)
    part = max(size for size in range(16, 512, 16) if cells % size == 0)
    for first in range(0, cells, part):
        rot_out[first:first + part] = jnp.dot(
            flat[first:first + part], whole, preferred_element_type=F32).astype(BF16)

    with scope('ham_2'):
        while ham_streams[0].phase < len(ham_plan[0][2]):
            end(ham_streams)
    last_h = last_sum(ham_streams, gx_h, ham_out)

    with scope('last'):
        last_c.wait_recv()
        last_h.wait_recv()
    for copy in sent + [pair_copy_c, pair_copy_h, pair_copy_e, last_c, last_h]:
        copy.wait_send()

    @pl.when(jnp.logical_not(last_y))
    def _():
        ahead.wait_send()

    @pl.when(jnp.logical_not(first_y))
    def _():
        back.wait_send()

    @pl.when(jnp.logical_not(last_x))
    def _():
        to_x.wait_send()

    assert copies.used == copy_count


def deliver(corr, ham, rot, corr_out, ham_out, rot_out, sems):
    copies = [pltpu.make_async_copy(source, target, sems.at[i]) for i, (source, target) in
              enumerate(((rot, rot_out), (corr, corr_out), (ham, ham_out)))]
    for copy in copies:
        copy.start()
    for copy in copies:
        copy.wait()


def in_hbm(array):
    return pltpu.with_memory_space_constraint(array, pltpu.HBM)


def on_device(bands, potential, eigenvectors):
    gx_size, gyz_size = lax.axis_size("gx"), lax.axis_size("gyz")
    cx, cy, cz, width = bands.shape
    rows = eigenvectors.shape[0]
    cells = cx * cy * cz
    sizes = digit_sizes(gyz_size)
    count = len(sizes)
    half = width // 2
    flat = bands.reshape(cells, width)
    ham_plan, corr_plan, coef_plan = plans_of(rows, sizes)
    orders = [order for _, _, order in ham_plan + corr_plan] + [coef_plan]
    copy_count = 3 + sum(copies_of(sizes, order) for order in orders) + 3 + 2 * (gx_size // 2)
    geometry = (gx_size, gyz_size, cx, cy, cz, width, rows, sizes, copy_count)

    buffers = []
    for first, last, order in ham_plan + corr_plan:
        outgoing, received, parts, left = [], [], [], list(range(count))
        for group in order:
            outgoing.append(pltpu.VMEM(tuple(sizes[i] for i in left) + (last - first, half), BF16))
            left = [d for d in left if d not in group]
            shape = tuple(sizes[i] for i in left) + (last - first, half)
            received.append(pltpu.VMEM((peer_count(sizes, group) - 1,) + shape, BF16))
            parts.append(pltpu.VMEM(shape, F32))
        buffers += outgoing + received + parts

    cut_x = (cx + 1) // 2
    ghosts = (cx + cy) * cz
    wide, narrow = sizes + (rows, width), sizes + (rows, half)
    others = max(gx_size // 2 - 1, 1)
    vmem, anywhere = pl.BlockSpec(memory_space=pltpu.VMEM), pl.BlockSpec(memory_space=pl.ANY)
    results = (jax.ShapeDtypeStruct((rows, width), F32), jax.ShapeDtypeStruct((rows, width), F32),
               jax.ShapeDtypeStruct((cells, width), BF16))
    computed = pl.pallas_call(
        functools.partial(kernel, geometry),
        out_shape=results,
        in_specs=[pl.BlockSpec(memory_space=pltpu.HBM)] * 4,
        out_specs=(vmem, vmem, vmem),
        scratch_shapes=[
            pltpu.VMEM((cells, width), BF16), pltpu.VMEM((cy, cx, cz), F32),
            pltpu.VMEM(wide, BF16),
            pltpu.VMEM((cells, width), F32), pltpu.VMEM((cells, width), BF16),
            pltpu.VMEM(wide, F32), pltpu.VMEM(wide, F32),
            pltpu.VMEM((cut_x, cz, width), BF16), pltpu.VMEM((cx - cut_x, cz, width), BF16),
            pltpu.VMEM((cy, cz, width), BF16),
            pltpu.VMEM((ghosts, width), BF16), pltpu.VMEM((ghosts, width), BF16),
            pltpu.VMEM(narrow, F32), pltpu.VMEM(narrow, F32),
            pltpu.VMEM(narrow, F32), pltpu.VMEM(narrow, F32),
            pltpu.VMEM((others, rows, half), F32), pltpu.VMEM((others, rows, half), F32),
            pltpu.SemaphoreType.DMA((copy_count,)), pltpu.SemaphoreType.DMA((copy_count,)),
            pltpu.SemaphoreType.DMA((3,)), *buffers,
        ],
        compiler_params=pltpu.CompilerParams(
            collective_id=0, has_side_effects=True, vmem_limit_bytes=52 * 1024 * 1024),
    )(bands, flat, in_hbm(jnp.transpose(potential, (1, 0, 2))), in_hbm(eigenvectors))
    corr, ham, rotated = pl.pallas_call(
        deliver, out_shape=results, in_specs=[vmem] * 3, out_specs=[anywhere] * 3,
        scratch_shapes=[pltpu.SemaphoreType.DMA((3,))],
        compiler_params=pltpu.CompilerParams(vmem_limit_bytes=8 * 1024 * 1024),
    )(*computed)
    return corr, ham, rotated.reshape(bands.shape)


def solution(mesh):
    in_specs = (P("gx", "gyz", None, None), P("gx", "gyz", None), P("gyz", None))
    out_specs = (P("gyz", None), P("gyz", None), P("gx", "gyz", None, None))
    return jax.shard_map(
        on_device, mesh=mesh, in_specs=in_specs, out_specs=out_specs, check_vma=False
    )
```

time: 33.1 us -> 28 us (0.85)
  the two profiles are of different devices: /device:TPU:0 before, /device:TPU:5 now
where the time goes in v1:
time: 28 us; the launch traced here: 27.8 us
  Pallas kernels  27.2 us (97%)
  between operations  0.64 us (2%)
    pallas_call x1, Pallas kernels, on_device(): pl.pallas_call(functools.partial(kernel, geometry), out_shape=results, in...  26 us
    pallas_call x1, Pallas kernels, on_device(): pl.pallas_call(deliver, out_shape=results, in_specs=[vmem] * 3, out_specs...  1.22 us

profile of v1, /device:TPU:5, one launch (start us, length us, event | category | flops | bytes accessed | tf_op | source)
XLA Modules:
  0.0 27.8 jit_solution(1869590202694116977)
XLA Ops:
  0.6 26.0 %shard_map.58 = (f32[32,512]{1,0:T(8,128)S(1)}, f32[32,512]{1,0:T(8,128)S(1)}, bf16[1600,512]{1,0:T(8,128)(2,1)S(1)}) custom-call(bf16[8,5,40,512]{3,2,1,0:T(8,128)(2,1)} %grid4.1, bf16[1600,512]{1,0:T(8,128)(2,1)} %bitcast.3, f32[5,8,40]{2,1,0:T(8,128)} %bitcast.4, bf16[32,512]{1,0:T(8,128)(2,1)} %eig.1), custom_call_target="tpu_custom_call" | custom-call | tf_op jit(solution)/shard_map/pallas_call | solution.py:454
  26.6 1.2 %shard_map.59 = (f32[32,512]{1,0:T(8,128)}, f32[32,512]{1,0:T(8,128)}, bf16[1600,512]{1,0:T(8,128)(2,1)}) custom-call(f32[32,512]{1,0:T(8,128)S(1)} %get-tuple-element.9.corr, f32[32,512]{1,0:T(8,128)S(1)} %get-tuple-element.10.ham, bf16[1600,512]{1,0:T(8,128)(2,1)S(1)} %get-tuple-element.11.rot), custom_call_target="tpu_custom_call" | custom-call | tf_op jit(solution)/shard_map/pallas_call | solution.py:476

commit v2 on v1

--- a/solution.py
+++ b/solution.py
@@ -1,6 +1,7 @@
 import functools
 import itertools
 import math
+import types
 
 import jax
 import jax.numpy as jnp
@@ -27,16 +28,43 @@
     return lax.dot_general(left, right, (((0,), (0,)), ((), ())), preferred_element_type=F32)
 
 
+class Group:
+    def __init__(self, send_sem, recv_sem):
+        self.send_sem, self.recv_sem, self.whole = send_sem, recv_sem, None
+
+    def start(self, src, dst, device_id):
+        pltpu.make_async_remote_copy(
+            src_ref=src, dst_ref=dst, send_sem=self.send_sem, recv_sem=self.recv_sem,
+            device_id=device_id, device_id_type=MESH).start()
+
+    def wait_recv(self):
+        pltpu.make_async_copy(self.whole, self.whole, self.recv_sem).wait()
+
+    def wait_send(self):
+        pltpu.make_async_copy(self.whole, self.whole, self.send_sem).wait()
+
+
 class Copies:
     def __init__(self, send_sems, recv_sems):
         self.send_sems, self.recv_sems, self.used = send_sems, recv_sems, 0
 
+    def slot(self):
+        self.used += 1
+        return self.send_sems.at[self.used - 1], self.recv_sems.at[self.used - 1]
+
     def make(self, src, dst, device_id):
-        slot = self.used
-        self.used += 1
+        send_sem, recv_sem = self.slot()
         return pltpu.make_async_remote_copy(
-            src_ref=src, dst_ref=dst, send_sem=self.send_sems.at[slot],
-            recv_sem=self.recv_sems.at[slot], device_id=device_id, device_id_type=MESH)
+            src_ref=src, dst_ref=dst, send_sem=send_sem, recv_sem=recv_sem,
+            device_id=device_id, device_id_type=MESH)
+
+    def group(self, whole):
+        made = Group(*self.slot())
+        made.whole = whole
+        return made
+
+
+Z, XY = (0, 1), (2, 3)
 
 
 def singles(order):
@@ -46,9 +74,8 @@
 def plans_of(rows, sizes):
     count = len(sizes)
     if sizes == (2, 2, 2, 2) and rows % 32 == 0:
-        ham = ((0, rows // 2, ((2, 3), (0, 1))), (rows // 2, rows, ((0, 1), (2, 3))))
-        corr = ((0, rows, ((0, 1), (2, 3))),)
-        return ham, corr, ((0, 1), (3,), (2,))
+        ham = ((0, rows // 2, (XY, Z)), (rows // 2, rows, (Z, XY)))
+        return ham, ((0, rows, (Z, XY)),), (Z, (3,), (2,))
     fast, slow = singles(range(count)[::-1]), singles(range(count))
     return ((0, rows, fast),), ((0, rows, slow),), slow
 
@@ -62,54 +89,114 @@
 
 
 class Stream:
-    def __init__(self, context, source, first, last, order, outgoing, received, parts):
-        self.context, self.source, self.order, self.outgoing = context, source, order, outgoing
-        self.rows, self.received, self.parts = slice(first, last), received, parts
-        self.left, self.phase = list(range(len(context[1]))), 0
+    def __init__(self, context, source, final, first, last, order, buffers):
+        self.context, self.source, self.final, self.order = context, source, final, order
+        self.rows, self.buffers = slice(first, last), buffers
+        self.left, self.phase = list(range(len(context.sizes))), 0
 
     def index(self, values):
-        at = tuple(values[d] if d in values else slice(None) for d in self.left)
-        return at
-
-    def current(self):
-        everything = tuple(slice(None) for _ in self.left)
-        return self.source[everything + (self.rows,)] if self.phase == 0 else self.source[...]
+        return tuple(values[d] if d in values else slice(None) for d in self.left)
+
+    def peers(self):
+        group = self.order[self.phase]
+        return [self.context.peer(group, k) for k in range(peer_count(self.context.sizes, group))]
+
+    def combos(self, fixed):
+        free = [d for d in self.left if d not in fixed]
+        for values in itertools.product(*(range(self.context.sizes[d]) for d in free)):
+            yield {**dict(zip(free, values)), **fixed}
+
+    def diagonal(self, values, parity):
+        ctx = self.context
+        block = sum(values.get(d, ctx.digits[d]) * ctx.strides[d] for d in range(len(ctx.sizes)))
+        shape = (self.rows.stop - self.rows.start, ctx.half)
+        row = lax.broadcasted_iota(jnp.int32, shape, 0) + (block * ctx.rows + self.rows.start)
+        return row == lax.broadcasted_iota(jnp.int32, shape, 1) + parity * ctx.half
+
+    def round(self, fixed):
+        out, extra = self.buffers[self.phase][:2]
+        for values in self.combos(fixed):
+            at = self.index(values)
+            value = self.source[at + (self.rows,) if self.phase == 0 else at]
+            short = value.astype(BF16)
+            out[at] = short
+            rest = jnp.where(self.diagonal(values, self.context.parity), value - short.astype(F32), 0.0)
+            extra[at] = jnp.sum(rest, axis=0, keepdims=True)
+
+    def open(self):
+        landing, extras = self.buffers[self.phase][2:4]
+        self.flights = self.context.copies.group(landing), self.context.copies.group(extras)
+
+    def ship(self, at, slot, device):
+        out, extra, landing, extras = self.buffers[self.phase][:4]
+        self.flights[0].start(out.at[at], landing.at[slot], device)
+        self.flights[1].start(extra.at[at], extras.at[slot], device)
+
+    def send(self, k):
+        target, values = self.peers()[k]
+        self.round(values)
+        self.ship(self.index(values), k - 1, (self.context.gx, target))
 
     def start(self):
-        copies, sizes, digits, gx, peer = self.context
-        group = self.order[self.phase]
-        self.flying = []
-        out = self.outgoing[self.phase]
-        out[...] = self.current().astype(BF16)
-        for k in range(1, peer_count(sizes, group)):
-            target, values = peer(group, k)
-            copy = copies.make(out.at[self.index(values)],
-                               self.received[self.phase].at[k - 1], (gx, target))
-            copy.start()
-            self.flying.append(copy)
+        self.open()
+        for k in range(1, len(self.peers())):
+            self.send(k)
+
+    def start_both(self):
+        self.open()
+        self.round({})
+        peers = self.peers()
+        for k, (target, values) in enumerate(peers):
+            at = self.index(values)
+            if k:
+                self.ship(at, k - 1, (self.context.gx, target))
+            self.ship(at, len(peers) - 1 + k, (self.context.partner, target))
+
+    def land(self):
+        for flight in self.flights:
+            flight.wait_recv()
+
+    def finish_both(self, columns, scale):
+        self.land()
+        out, extra, landing, extras = self.buffers[self.phase][:4]
+        many = len(self.peers())
+        at = self.index(self.peers()[0][1])
+        mine = [(out[at], extra[at])] + [(landing[k], extras[k]) for k in range(many - 1)]
+        across = [(landing[k], extras[k]) for k in range(many - 1, 2 * many - 1)]
+        parity = self.context.parity
+        for column, side, parts in zip(columns, (parity, 1 - parity), (mine, across)):
+            total = sum(part.astype(F32) for part, _ in parts)
+            rest = sum(rest for _, rest in parts)
+            total = total + jnp.where(self.diagonal({}, side), rest, 0.0)
+            self.final[self.rows, column] = total * scale
+        self.phase += 1
 
     def finish(self):
-        copies, sizes, digits, gx, peer = self.context
-        group = self.order[self.phase]
-        for copy in self.flying:
-            copy.wait_recv()
-        own = self.index({d: digits[d] for d in group})
-        total = self.source[own + (self.rows,) if self.phase == 0 else own]
-        for k in range(1, peer_count(sizes, group)):
-            total = total + self.received[self.phase][k - 1].astype(F32)
-        self.parts[self.phase][...] = total
-        self.source = self.parts[self.phase]
-        self.left = [d for d in self.left if d not in group]
+        self.land()
+        _, _, landing, extras, result = self.buffers[self.phase]
+        own = self.peers()[0][1]
+        for values in self.combos(own):
+            at = self.index(values)
+            total = self.source[at + (self.rows,) if self.phase == 0 else at]
+            keep = tuple(values[d] for d in self.left if d not in own)
+            rest = 0.0
+            for k in range(landing.shape[0]):
+                total = total + landing[(k,) + keep].astype(F32)
+                rest = rest + extras[(k,) + keep]
+            result[keep + (Ellipsis,)] = total + jnp.where(self.diagonal(values, self.context.parity), rest, 0.0)
+        self.source = result
+        self.left = [d for d in self.left if d not in own]
         self.phase += 1
 
 
 def kernel(geometry, grid4, rows_in, pot_in, eig, corr_out, ham_out, rot_out, flat, pot, coef, padded, hq,
-           corr, ham, halo_f, halo_b, halo_x, own, ghost, pair_c, pair_h, sum_c, sum_h, gx_c, gx_h,
+           corr, ham, halo_f, halo_b, halo_x, face, turned, ghosts, late, pair_l, pair_c, pair_h, sum_c, sum_h, gx_c, gx_h,
            send_sems, recv_sems, local_sems, *buffers):
     gx_size, gyz_size, cx, cy, cz, bands, rows, sizes, copy_count = geometry
     ham_plan, corr_plan, coef_plan = plans_of(rows, sizes)
     count = len(sizes)
     half = bands // 2
+    relayed, direct = sizes == (2, 2, 2, 2), gx_size == 2
     gx, gyz = lax.axis_index("gx"), lax.axis_index("gyz")
     parity = lax.rem(gx, 2)
     partner = gx + 1 - 2 * parity
@@ -149,6 +236,9 @@
             pl.semaphore_signal(barrier, inc=1, device_id=device, device_id_type=MESH)
     neighbours = sum(1 - edge.astype(jnp.int32) for edge, _ in beside)
     greeted = []
+    if direct:
+        for group in sorted({order[-1] for _, _, order in ham_plan + corr_plan}):
+            greeted += [(partner, peer(group, k)[0]) for k in range(1, peer_count(sizes, group))]
     groups = []
     for _, _, order in ham_plan + corr_plan + ((0, 0, coef_plan),):
         groups += [group for group in order if group not in groups]
@@ -163,23 +253,60 @@
 
     sent = []
 
-    def coef_phase(at):
+    def coef_send(group, held):
         started = []
-        done = {d for group in coef_plan[:at] for d in group}
-        index = tuple(slice(None) if d in done else digits[d] for d in range(count)) + (slice(None), mine)
-        for k in range(1, peer_count(sizes, coef_plan[at])):
-            block = coef.at[index]
-            copy = copies.make(block, block, (gx, peer(coef_plan[at], k)[0]))
-            copy.start()
-            started.append(copy)
+        for k in range(1, peer_count(sizes, group)):
+            block = coef.at[held + (slice(None), mine)]
+            started.append(copies.make(block, block, (gx, peer(group, k)[0])))
+            started[-1].start()
         sent.extend(started)
         return started
 
-    def next_coef_phase(started, at):
-        for copy in started:
+    def coef_held(groups):
+        done = {d for group in groups for d in group}
+        return tuple(slice(None) if d in done else digits[d] for d in range(count))
+
+    def coef_exchange():
+        block = coef.at[tuple([slice(None)] * (count + 1)) + (mine,)]
+        coef_state[2] = copies.make(block, block, (partner, gyz))
+        coef_state[2].start()
+
+    def coef_wait(flying):
+        for copy in flying:
             copy.wait_recv()
-        return coef_phase(at) if at < len(coef_plan) else []
-
+
+    def coef_start():
+        coef_state[1] = coef_send(coef_plan[0], coef_held(()))
+
+    coef_steps = 4 if relayed else len(coef_plan)
+
+    def coef_step():
+        state, at = coef_state, coef_state[0]
+        state[0] += 1
+        with scope("coef_%d" % at):
+            if not relayed:
+                coef_wait(state[1])
+                if at + 1 < len(coef_plan):
+                    state[1] = coef_send(coef_plan[at + 1], coef_held(coef_plan[:at + 1]))
+                else:
+                    coef_exchange()
+                return
+            held = coef_held(coef_plan[:-2])
+            if at == 0:
+                coef_wait(state[1])
+                state[3] = coef_send(coef_plan[-1], held)
+            elif at == 1:
+                state[1] = coef_send(coef_plan[-2], held)
+            elif at == 2:
+                coef_wait(state[1])
+                d, = coef_plan[-2]
+                state[3] += coef_send(coef_plan[-1], held[:d] + (1 - digits[d],) + held[d + 1:])
+            else:
+                coef_wait(state[3])
+                coef_exchange()
+
+    coef_state = [0, None, None, []]
+    load_coef.wait()
 
     to_x = copies.make(grid4.at[cx - 1], halo_x, (lax.rem(gx + 1, gx_size), gyz))
     cut_x = (cx + 1) // 2
@@ -210,8 +337,7 @@
     def _():
         halo_b[...] = jnp.zeros_like(halo_b)
 
-    load_coef.wait()
-    coef_copies = coef_phase(0)
+    coef_start()
 
     def block_index(block):
         index = []
@@ -260,19 +386,18 @@
         hq[first * cz:(first + per) * cz] = jnp.concatenate(
             [segment(*xy) for xy in order[first:first + per]]).astype(BF16)
 
-    context = (copies, sizes, digits, gx, peer)
+    context = types.SimpleNamespace(
+        copies=copies, sizes=sizes, digits=digits, strides=strides, peer=peer, gx=gx, partner=partner,
+        parity=parity, rows=rows, half=half)
     taken = iter(buffers)
 
-    def streams(plan, source):
-        made = []
-        for first, last, digit_order in plan:
-            outgoing = [next(taken) for _ in digit_order]
-            received = [next(taken) for _ in digit_order]
-            parts = [next(taken) for _ in digit_order]
-            made.append(Stream(context, source, first, last, digit_order, outgoing, received, parts))
-        return made
-
-    ham_streams, corr_streams = streams(ham_plan, sum_h), streams(corr_plan, sum_c)
+    scale = 1.0 / (cells * gyz_size)
+
+    def streams(plan, source, final):
+        return [Stream(context, source, final, first, last, order, [[next(taken) for _ in range(5)] for _ in order])
+                for first, last, order in plan]
+
+    ham_streams, corr_streams = streams(ham_plan, sum_h, ham_out), streams(corr_plan, sum_c, corr_out)
 
     def begin(group):
         for stream in group:
@@ -280,9 +405,15 @@
 
     def end(group):
         for stream in group:
+            if direct and stream.phase == len(stream.order) - 1:
+                stream.finish_both((mine, other), scale)
+                sent.extend(stream.flights)
+                continue
             stream.finish()
-            sent.extend(stream.flying)
-            if stream.phase < len(stream.order):
+            sent.extend(stream.flights)
+            if direct and stream.phase == len(stream.order) - 1:
+                stream.start_both()
+            elif stream.phase < len(stream.order):
                 stream.start()
 
     with scope('pair_c'):
@@ -290,50 +421,92 @@
     sum_c[...] = corr[everything + (mine,)] + pair_c[...]
     begin(corr_streams)
 
+    def corr_step():
+        at = corr_streams[0].phase
+        with scope("corr_%d" % at):
+            end(corr_streams)
+
     for first in range(0, bands, tile):
         store_rows(ham, first, gram_t(flat[:, first:first + tile], hq[...]))
 
-    own[...] = jnp.concatenate(
-        [flat[x * plane:x * plane + cz] for x in range(cut_x)]
-        + [flat[x * plane + plane - cz:x * plane + plane] for x in range(cut_x, cx)] + [flat[0:plane]])
-
-    with scope('halo'):
+    def add_cross(target, column, value):
+        for j in range(bands // rows):
+            index = block_index(j) + (slice(None), column)
+            target[index] = target[index] - 0.5 * value[j * rows:(j + 1) * rows]
+
+    faces = []
+    for at, (cells_x, y) in enumerate(((range(cut_x), 0), (range(cut_x, cx), cy - 1))):
+        own = jnp.concatenate([flat[x * plane + y * cz:x * plane + y * cz + cz] for x in cells_x])
+        face[at, 0:own.shape[0]] = own
+        turned[at, :, 0:own.shape[0]] = jnp.transpose(own)
+        faces.append((face.at[at, 0:own.shape[0]], turned.at[at, :, 0:own.shape[0]]))
+
+    @pl.when(jnp.logical_not(first_x))
+    def _():
+        to_x.wait_recv()
+
+    near, far = flat[0:plane], jnp.concatenate([halo_x[y] for y in range(cy)])
+    for first in range(0, bands, tile):
+        cut = slice(first, first + tile)
+        add_cross(ham, cut, gram_t(near, far[:, cut]) + gram_t(far, near[:, cut]))
+
+    with scope('ahead'):
         @pl.when(jnp.logical_not(first_y))
         def _():
             ahead.wait_recv()
 
+    ghosts[0:cut_x * cz] = jnp.concatenate([halo_f[x] for x in range(cut_x)])
+    forward = ghosts.at[0:cut_x * cz]
+    forward_t = jnp.transpose(forward[...])
+    backward = ghosts.at[cut_x * cz:cx * cz]
+
+    def cross(at, ghost, ghost_t, column):
+        near, near_t = faces[at]
+        return (jnp.dot(near_t[...], ghost[:, column], preferred_element_type=F32)
+                + jnp.dot(ghost_t, near[:, column], preferred_element_type=F32))
+
+    def add(column, value):
+        add_cross(ham, column, value)
+
+    add(other, cross(0, forward, forward_t, other))
+    pair_copy_h = copies.make(ham.at[everything + (other,)], pair_h, (partner, gyz))
+    pair_copy_h.start()
+    add(mine, cross(0, forward, forward_t, mine))
+
+    if coef_state[0] < coef_steps:
+        coef_step()
+    with scope('back'):
         @pl.when(jnp.logical_not(last_y))
         def _():
             back.wait_recv()
 
-        @pl.when(jnp.logical_not(first_x))
-        def _():
-            to_x.wait_recv()
-
-    with scope('coef_z'):
-        coef_copies = next_coef_phase(coef_copies, 1)
-
-    ghost[...] = jnp.concatenate(
-        [halo_f[x] for x in range(cut_x)] + [halo_b[x] for x in range(cx - cut_x)]
-        + [halo_x[y] for y in range(cy)])
-    cross = padded.at[0:bands]
-    for first in range(0, bands, tile):
-        cut = slice(first, first + tile)
-        cross[cut] = -0.5 * gram_t(own[:, cut], ghost[...])
-    for first in range(0, bands, tile):
-        cut = slice(first, first + tile)
-        value = cross[cut] + jnp.transpose(cross[:, cut])
-        for j in range(tile // rows):
-            index = block_index(first // rows + j)
-            ham[index] = ham[index] + value[j * rows:(j + 1) * rows]
-    pair_copy_h = copies.make(ham.at[everything + (other,)], pair_h, (partner, gyz))
-    pair_copy_h.start()
+    if coef_state[0] < coef_steps:
+        coef_step()
+    ghosts[cut_x * cz:cx * cz] = jnp.concatenate([halo_b[x] for x in range(cx - cut_x)])
+    backward_t = jnp.transpose(backward[...])
+    value = cross(1, backward, backward_t, other)
+    for j in range(bands // rows):
+        late[block_index(j)] = (-0.5 * value[j * rows:(j + 1) * rows]).astype(BF16)
+    pieces = [(ham_streams[0], k, at) for k, at in enumerate(ham_streams[0].index(values) for _, values in ham_streams[0].peers())]
+    pieces = pieces[1:] + [(stream, None, everything[:-1]) for stream in ham_streams[1:]] + pieces[:1]
+    pair_copies_h = []
+    for stream, k, at in pieces:
+        at = at + (stream.rows,)
+        copy = copies.make(late.at[at], pair_l.at[at], (partner, gyz))
+        copy.start()
+        pair_copies_h.append(copy)
+    add(mine, cross(1, backward, backward_t, mine))
     with scope('pair_h'):
+        ham_streams[0].open()
         pair_copy_h.wait_recv()
-    sum_h[...] = ham[everything + (mine,)] + pair_h[...]
-    begin(ham_streams)
-
-    scale = 1.0 / (cells * gyz_size)
+        for (stream, k, at), copy in zip(pieces, pair_copies_h):
+            at = at + (stream.rows,)
+            copy.wait_recv()
+            sum_h[at] = ham[at + (mine,)] + pair_h[at] + pair_l[at].astype(F32)
+            if k is None:
+                stream.start()
+            elif k:
+                stream.send(k)
 
     def last_sum(group, gx_recv, final):
         for at, stream in enumerate(group):
@@ -354,41 +527,45 @@
         copy.start()
         return copy
 
-    coef_steps = len(coef_plan)
-    with scope('corr_1'):
-        end(corr_streams)
-    with scope('coef_x'):
-        if coef_steps > 2:
-            coef_copies = next_coef_phase(coef_copies, 2)
-    with scope('ham_1'):
-        end(ham_streams)
-    with scope('coef_y'):
-        for at in range(min(coef_steps, 3), coef_steps + 1):
-            coef_copies = next_coef_phase(coef_copies, at)
-    mine_block = coef.at[everything + (mine,)]
-    pair_copy_e = copies.make(mine_block, mine_block, (partner, gyz))
-    pair_copy_e.start()
-    with scope('corr_2'):
-        while corr_streams[0].phase < len(corr_plan[0][2]):
-            end(corr_streams)
-    last_c = last_sum(corr_streams, gx_c, corr_out)
-    with scope('pair_e'):
-        pair_copy_e.wait_recv()
-    whole = coef[...].reshape(bands, bands)
     part = max(size for size in range(16, 512, 16) if cells % size == 0)
-    for first in range(0, cells, part):
-        rot_out[first:first + part] = jnp.dot(
-            flat[first:first + part], whole, preferred_element_type=F32).astype(BF16)
-
-    with scope('ham_2'):
-        while ham_streams[0].phase < len(ham_plan[0][2]):
-            end(ham_streams)
-    last_h = last_sum(ham_streams, gx_h, ham_out)
+
+    def rotate(column):
+        some = coef[everything + (column,)].reshape(bands, half)
+        for first in range(0, cells, part):
+            rot_out[first:first + part, column] = jnp.dot(
+                flat[first:first + part], some, preferred_element_type=F32).astype(BF16)
+
+    last = []
+    if relayed:
+        steps = ["corr", "coef", "ham", "coef", "rot", "corr", "ham"]
+    else:
+        steps = ["coef"] * (coef_steps - coef_state[0]) + ["rot"]
+        steps += ["corr"] * len(corr_plan[0][2]) + ["ham"] * len(ham_plan[0][2])
+    for step in steps:
+        if step == "corr":
+            corr_step()
+            if corr_streams[0].phase == len(corr_streams[0].order):
+                last += [] if direct else [last_sum(corr_streams, gx_c, corr_out)]
+        if step == "ham":
+            at = ham_streams[0].phase
+            with scope("ham_%d" % at):
+                for stream in ham_streams:
+                    end([stream])
+            if ham_streams[0].phase == len(ham_streams[0].order):
+                last += [] if direct else [last_sum(ham_streams, gx_h, ham_out)]
+        if step == "coef":
+            coef_step()
+        if step == "rot":
+            rotate(mine)
+            with scope("pair_e"):
+                coef_state[2].wait_recv()
+            rotate(other)
+    pair_copy_e = coef_state[2]
 
     with scope('last'):
-        last_c.wait_recv()
-        last_h.wait_recv()
-    for copy in sent + [pair_copy_c, pair_copy_h, pair_copy_e, last_c, last_h]:
+        for copy in last:
+            copy.wait_recv()
+    for copy in sent + pair_copies_h + [pair_copy_c, pair_copy_h, pair_copy_e] + last:
         copy.wait_send()
 
     @pl.when(jnp.logical_not(last_y))
@@ -429,23 +606,27 @@
     half = width // 2
     flat = bands.reshape(cells, width)
     ham_plan, corr_plan, coef_plan = plans_of(rows, sizes)
-    orders = [order for _, _, order in ham_plan + corr_plan] + [coef_plan]
-    copy_count = 3 + sum(copies_of(sizes, order) for order in orders) + 3 + 2 * (gx_size // 2)
+    copy_count = 7 + peer_count(sizes, ham_plan[0][2][0]) + len(ham_plan) - 1
+    copy_count += sum(2 * len(order) for _, _, order in ham_plan + corr_plan)
+    copy_count += copies_of(sizes, coef_plan) + (sizes == (2, 2, 2, 2)) - 1
+    copy_count += 0 if gx_size == 2 else 2 * (gx_size // 2)
     geometry = (gx_size, gyz_size, cx, cy, cz, width, rows, sizes, copy_count)
 
     buffers = []
     for first, last, order in ham_plan + corr_plan:
-        outgoing, received, parts, left = [], [], [], list(range(count))
+        left = list(range(count))
         for group in order:
-            outgoing.append(pltpu.VMEM(tuple(sizes[i] for i in left) + (last - first, half), BF16))
+            many = peer_count(sizes, group)
+            many = 2 * many - 1 if gx_size == 2 and group == order[-1] else many - 1
+            whole = tuple(sizes[i] for i in left)
             left = [d for d in left if d not in group]
-            shape = tuple(sizes[i] for i in left) + (last - first, half)
-            received.append(pltpu.VMEM((peer_count(sizes, group) - 1,) + shape, BF16))
-            parts.append(pltpu.VMEM(shape, F32))
-        buffers += outgoing + received + parts
+            kept = tuple(sizes[i] for i in left)
+            cut, line = (last - first, half), (1, half)
+            buffers += [pltpu.VMEM(whole + cut, BF16), pltpu.VMEM(whole + line, F32),
+                        pltpu.VMEM((many,) + kept + cut, BF16), pltpu.VMEM((many,) + kept + line, F32),
+                        pltpu.VMEM(kept + cut, F32)]
 
     cut_x = (cx + 1) // 2
-    ghosts = (cx + cy) * cz
     wide, narrow = sizes + (rows, width), sizes + (rows, half)
     others = max(gx_size // 2 - 1, 1)
     vmem, anywhere = pl.BlockSpec(memory_space=pltpu.VMEM), pl.BlockSpec(memory_space=pl.ANY)
@@ -463,7 +644,8 @@
             pltpu.VMEM(wide, F32), pltpu.VMEM(wide, F32),
             pltpu.VMEM((cut_x, cz, width), BF16), pltpu.VMEM((cx - cut_x, cz, width), BF16),
             pltpu.VMEM((cy, cz, width), BF16),
-            pltpu.VMEM((ghosts, width), BF16), pltpu.VMEM((ghosts, width), BF16),
+            pltpu.VMEM((2, cut_x * cz, width), BF16), pltpu.VMEM((2, width, cut_x * cz), BF16),
+            pltpu.VMEM((cx * cz, width), BF16), pltpu.VMEM(narrow, BF16), pltpu.VMEM(narrow, BF16),
             pltpu.VMEM(narrow, F32), pltpu.VMEM(narrow, F32),
             pltpu.VMEM(narrow, F32), pltpu.VMEM(narrow, F32),
             pltpu.VMEM((others, rows, half), F32), pltpu.VMEM((others, rows, half), F32),

time: 28 us -> 27.6 us (0.986)
  the two profiles are of different devices: /device:TPU:5 before, /device:TPU:0 now
where the time goes in v2:
time: 27.6 us; the launch traced here: 27.5 us
  Pallas kernels  26.8 us (97%)
  between operations  0.64 us (2%)
    pallas_call x1, Pallas kernels, on_device(): pl.pallas_call(functools.partial(kernel, geometry), out_shape=results, in...  25.6 us
    pallas_call x1, Pallas kernels, on_device(): pl.pallas_call(deliver, out_shape=results, in_specs=[vmem] * 3, out_specs...  1.22 us

profile of v2, /device:TPU:0, one launch (start us, length us, event | category | flops | bytes accessed | tf_op | source)
XLA Modules:
  0.0 27.5 jit_solution(10136663439775542664)
XLA Ops:
  0.6 25.6 %shard_map.58 = (f32[32,512]{1,0:T(8,128)S(1)}, f32[32,512]{1,0:T(8,128)S(1)}, bf16[1600,512]{1,0:T(8,128)(2,1)S(1)}) custom-call(bf16[8,5,40,512]{3,2,1,0:T(8,128)(2,1)} %grid4.1, bf16[1600,512]{1,0:T(8,128)(2,1)} %bitcast.3, f32[5,8,40]{2,1,0:T(8,128)} %bitcast.4, bf16[32,512]{1,0:T(8,128)(2,1)} %eig.1), custom_call_target="tpu_custom_call" | custom-call | tf_op jit(solution)/shard_map/pallas_call | solution.py:635
  26.2 1.2 %shard_map.59 = (f32[32,512]{1,0:T(8,128)}, f32[32,512]{1,0:T(8,128)}, bf16[1600,512]{1,0:T(8,128)(2,1)}) custom-call(f32[32,512]{1,0:T(8,128)S(1)} %get-tuple-element.9.corr, f32[32,512]{1,0:T(8,128)S(1)} %get-tuple-element.10.ham, bf16[1600,512]{1,0:T(8,128)(2,1)S(1)} %get-tuple-element.11.rot), custom_call_target="tpu_custom_call" | custom-call | tf_op jit(solution)/shard_map/pallas_call | solution.py:658

commit v3 on v2

--- a/solution.py
+++ b/solution.py
@@ -28,40 +28,48 @@
     return lax.dot_general(left, right, (((0,), (0,)), ((), ())), preferred_element_type=F32)
 
 
+def bytes_of(ref):
+    return math.prod(ref.shape) * (2 if ref.dtype == BF16 else 4)
+
+
 class Group:
-    def __init__(self, send_sem, recv_sem):
-        self.send_sem, self.recv_sem, self.whole = send_sem, recv_sem, None
+    def __init__(self, copies, send_sem, recv_sem, whole):
+        self.copies, self.send_sem, self.recv_sem, self.whole = copies, send_sem, recv_sem, whole
 
     def start(self, src, dst, device_id):
+        self.copies.sent[self.send_sem] += bytes_of(src)
         pltpu.make_async_remote_copy(
-            src_ref=src, dst_ref=dst, send_sem=self.send_sem, recv_sem=self.recv_sem,
-            device_id=device_id, device_id_type=MESH).start()
+            src_ref=src, dst_ref=dst, send_sem=self.copies.send_sems.at[self.send_sem],
+            recv_sem=self.recv_sem, device_id=device_id, device_id_type=MESH).start()
 
     def wait_recv(self):
         pltpu.make_async_copy(self.whole, self.whole, self.recv_sem).wait()
 
-    def wait_send(self):
-        pltpu.make_async_copy(self.whole, self.whole, self.send_sem).wait()
-
 
 class Copies:
-    def __init__(self, send_sems, recv_sems):
-        self.send_sems, self.recv_sems, self.used = send_sems, recv_sems, 0
-
-    def slot(self):
+    def __init__(self, send_sems, recv_sems, measures):
+        self.send_sems, self.recv_sems, self.measures = send_sems, recv_sems, measures
+        self.used, self.sent = 0, [0, 0]
+
+    def group(self, whole, kind=0):
         self.used += 1
-        return self.send_sems.at[self.used - 1], self.recv_sems.at[self.used - 1]
-
-    def make(self, src, dst, device_id):
-        send_sem, recv_sem = self.slot()
-        return pltpu.make_async_remote_copy(
-            src_ref=src, dst_ref=dst, send_sem=send_sem, recv_sem=recv_sem,
-            device_id=device_id, device_id_type=MESH)
-
-    def group(self, whole):
-        made = Group(*self.slot())
-        made.whole = whole
+        return Group(self, kind, self.recv_sems.at[self.used - 1], whole)
+
+    def span(self, size, kind=0):
+        measure = self.measures[kind]
+        row = bytes_of(measure) // measure.shape[0]
+        assert size % row == 0 and size // row <= measure.shape[0]
+        return measure.at[0:size // row]
+
+    def start(self, src, dst, device_id):
+        made = self.group(dst)
+        made.start(src, dst, device_id)
         return made
+
+    def wait_sends(self):
+        for kind, size in enumerate(self.sent):
+            whole = self.span(size, kind)
+            pltpu.make_async_copy(whole, whole, self.send_sems.at[kind]).wait()
 
 
 Z, XY = (0, 1), (2, 3)
@@ -125,7 +133,7 @@
 
     def open(self):
         landing, extras = self.buffers[self.phase][2:4]
-        self.flights = self.context.copies.group(landing), self.context.copies.group(extras)
+        self.flights = self.context.copies.group(landing), self.context.copies.group(extras, 1)
 
     def ship(self, at, slot, device):
         out, extra, landing, extras = self.buffers[self.phase][:4]
@@ -191,7 +199,7 @@
 
 def kernel(geometry, grid4, rows_in, pot_in, eig, corr_out, ham_out, rot_out, flat, pot, coef, padded, hq,
            corr, ham, halo_f, halo_b, halo_x, face, turned, ghosts, late, pair_l, pair_c, pair_h, sum_c, sum_h, gx_c, gx_h,
-           send_sems, recv_sems, local_sems, *buffers):
+           span, lines, send_sems, recv_sems, local_sems, *buffers):
     gx_size, gyz_size, cx, cy, cz, bands, rows, sizes, copy_count = geometry
     ham_plan, corr_plan, coef_plan = plans_of(rows, sizes)
     count = len(sizes)
@@ -208,7 +216,7 @@
         step //= size
         strides.append(step)
     digits = [lax.rem(gyz // stride, size) for stride, size in zip(strides, sizes)]
-    copies = Copies(send_sems, recv_sems)
+    copies = Copies(send_sems, recv_sems, (span, lines))
 
     def peer(group, k):
         target, values = gyz, {}
@@ -236,9 +244,6 @@
             pl.semaphore_signal(barrier, inc=1, device_id=device, device_id_type=MESH)
     neighbours = sum(1 - edge.astype(jnp.int32) for edge, _ in beside)
     greeted = []
-    if direct:
-        for group in sorted({order[-1] for _, _, order in ham_plan + corr_plan}):
-            greeted += [(partner, peer(group, k)[0]) for k in range(1, peer_count(sizes, group))]
     groups = []
     for _, _, order in ham_plan + corr_plan + ((0, 0, coef_plan),):
         groups += [group for group in order if group not in groups]
@@ -251,16 +256,13 @@
     with scope("barrier"):
         pl.semaphore_wait(barrier, len(greeted) + neighbours)
 
-    sent = []
-
     def coef_send(group, held):
-        started = []
-        for k in range(1, peer_count(sizes, group)):
-            block = coef.at[held + (slice(None), mine)]
-            started.append(copies.make(block, block, (gx, peer(group, k)[0])))
-            started[-1].start()
-        sent.extend(started)
-        return started
+        many = peer_count(sizes, group) - 1
+        block = coef.at[held + (slice(None), mine)]
+        made = copies.group(copies.span(many * bytes_of(block)))
+        for k in range(1, many + 1):
+            made.start(block, block, (gx, peer(group, k)[0]))
+        return [made]
 
     def coef_held(groups):
         done = {d for group in groups for d in group}
@@ -268,8 +270,7 @@
 
     def coef_exchange():
         block = coef.at[tuple([slice(None)] * (count + 1)) + (mine,)]
-        coef_state[2] = copies.make(block, block, (partner, gyz))
-        coef_state[2].start()
+        coef_state[2] = copies.start(block, block, (partner, gyz))
 
     def coef_wait(flying):
         for copy in flying:
@@ -308,10 +309,15 @@
     coef_state = [0, None, None, []]
     load_coef.wait()
 
-    to_x = copies.make(grid4.at[cx - 1], halo_x, (lax.rem(gx + 1, gx_size), gyz))
+    def halo(at, src, dst, device_id):
+        return pltpu.make_async_remote_copy(
+            src_ref=src, dst_ref=dst, send_sem=send_sems.at[at + 2], recv_sem=recv_sems.at[copy_count + at],
+            device_id=device_id, device_id_type=MESH)
+
+    to_x = halo(0, grid4.at[cx - 1], halo_x, (lax.rem(gx + 1, gx_size), gyz))
     cut_x = (cx + 1) // 2
-    ahead = copies.make(grid4.at[:cut_x, cy - 1], halo_f, (gx, lax.rem(gyz + 1, gyz_size)))
-    back = copies.make(grid4.at[cut_x:, 0], halo_b, (gx, lax.rem(gyz + gyz_size - 1, gyz_size)))
+    ahead = halo(1, grid4.at[:cut_x, cy - 1], halo_f, (gx, lax.rem(gyz + 1, gyz_size)))
+    back = halo(2, grid4.at[cut_x:, 0], halo_b, (gx, lax.rem(gyz + gyz_size - 1, gyz_size)))
 
     @pl.when(jnp.logical_not(last_y))
     def _():
@@ -356,8 +362,7 @@
     for first in range(0, bands, tile):
         store_rows(corr, first, gram_t(flat[:, first:first + tile], flat[...]))
     everything = tuple([slice(None)] * (count + 1))
-    pair_copy_c = copies.make(corr.at[everything + (other,)], pair_c, (partner, gyz))
-    pair_copy_c.start()
+    pair_copy_c = copies.start(corr.at[everything + (other,)], pair_c, (partner, gyz))
     load_pot.wait()
 
     plane = cy * cz
@@ -405,12 +410,12 @@
 
     def end(group):
         for stream in group:
+            if stream.phase == len(stream.order):
+                continue
             if direct and stream.phase == len(stream.order) - 1:
                 stream.finish_both((mine, other), scale)
-                sent.extend(stream.flights)
                 continue
             stream.finish()
-            sent.extend(stream.flights)
             if direct and stream.phase == len(stream.order) - 1:
                 stream.start_both()
             elif stream.phase < len(stream.order):
@@ -469,8 +474,7 @@
         add_cross(ham, column, value)
 
     add(other, cross(0, forward, forward_t, other))
-    pair_copy_h = copies.make(ham.at[everything + (other,)], pair_h, (partner, gyz))
-    pair_copy_h.start()
+    pair_copy_h = copies.start(ham.at[everything + (other,)], pair_h, (partner, gyz))
     add(mine, cross(0, forward, forward_t, mine))
 
     if coef_state[0] < coef_steps:
@@ -492,9 +496,7 @@
     pair_copies_h = []
     for stream, k, at in pieces:
         at = at + (stream.rows,)
-        copy = copies.make(late.at[at], pair_l.at[at], (partner, gyz))
-        copy.start()
-        pair_copies_h.append(copy)
+        pair_copies_h.append(copies.start(late.at[at], pair_l.at[at], (partner, gyz)))
     add(mine, cross(1, backward, backward_t, mine))
     with scope('pair_h'):
         ham_streams[0].open()
@@ -509,23 +511,17 @@
                 stream.send(k)
 
     def last_sum(group, gx_recv, final):
-        for at, stream in enumerate(group):
-            final[stream.rows, mine] = stream.source[...]
-        others = []
+        total, others = group[0].source, []
         for k in range(1, gx_size // 2):
             target = (lax.rem(gx + 2 * k, gx_size), gyz)
-            copy = copies.make(final.at[:, mine], gx_recv.at[k - 1], target)
-            copy.start()
-            others.append(copy)
+            others.append(copies.start(total, gx_recv.at[k - 1], target))
         for copy in others:
-            copy.wait()
-        total = final[:, mine]
+            copy.wait_recv()
+        total = total[...]
         for k in range(1, gx_size // 2):
             total = total + gx_recv[k - 1]
         final[:, mine] = total * scale
-        copy = copies.make(final.at[:, mine], final.at[:, mine], (partner, gyz))
-        copy.start()
-        return copy
+        return copies.start(final.at[:, mine], final.at[:, mine], (partner, gyz))
 
     part = max(size for size in range(16, 512, 16) if cells % size == 0)
 
@@ -548,8 +544,8 @@
                 last += [] if direct else [last_sum(corr_streams, gx_c, corr_out)]
         if step == "ham":
             at = ham_streams[0].phase
-            with scope("ham_%d" % at):
-                for stream in ham_streams:
+            for which, stream in enumerate(ham_streams):
+                with scope("ham%d_%d" % (which, at)):
                     end([stream])
             if ham_streams[0].phase == len(ham_streams[0].order):
                 last += [] if direct else [last_sum(ham_streams, gx_h, ham_out)]
@@ -560,13 +556,10 @@
             with scope("pair_e"):
                 coef_state[2].wait_recv()
             rotate(other)
-    pair_copy_e = coef_state[2]
-
     with scope('last'):
         for copy in last:
             copy.wait_recv()
-    for copy in sent + pair_copies_h + [pair_copy_c, pair_copy_h, pair_copy_e] + last:
-        copy.wait_send()
+    copies.wait_sends()
 
     @pl.when(jnp.logical_not(last_y))
     def _():
@@ -606,9 +599,9 @@
     half = width // 2
     flat = bands.reshape(cells, width)
     ham_plan, corr_plan, coef_plan = plans_of(rows, sizes)
-    copy_count = 7 + peer_count(sizes, ham_plan[0][2][0]) + len(ham_plan) - 1
+    copy_count = 4 + peer_count(sizes, ham_plan[0][2][0]) + len(ham_plan) - 1
     copy_count += sum(2 * len(order) for _, _, order in ham_plan + corr_plan)
-    copy_count += copies_of(sizes, coef_plan) + (sizes == (2, 2, 2, 2)) - 1
+    copy_count += len(coef_plan) + (sizes == (2, 2, 2, 2)) - 1
     copy_count += 0 if gx_size == 2 else 2 * (gx_size // 2)
     geometry = (gx_size, gyz_size, cx, cy, cz, width, rows, sizes, copy_count)
 
@@ -649,7 +642,8 @@
             pltpu.VMEM(narrow, F32), pltpu.VMEM(narrow, F32),
             pltpu.VMEM(narrow, F32), pltpu.VMEM(narrow, F32),
             pltpu.VMEM((others, rows, half), F32), pltpu.VMEM((others, rows, half), F32),
-            pltpu.SemaphoreType.DMA((copy_count,)), pltpu.SemaphoreType.DMA((copy_count,)),
+            pltpu.VMEM((cells * width // 1024, 8, 128), F32), pltpu.VMEM((256, 1, half), F32),
+            pltpu.SemaphoreType.DMA((5,)), pltpu.SemaphoreType.DMA((copy_count + 3,)),
             pltpu.SemaphoreType.DMA((3,)), *buffers,
         ],
         compiler_params=pltpu.CompilerParams(

time: 27.6 us -> 27.1 us (0.982)
  Pallas kernels: 26.8 us -> 26.3 us
    pallas_call x1, Pallas kernels: 25.6 us -> 25.1 us  [on_device(): pl.pallas_call(functools.partial(kernel, geometry), out_shape=results, in...]
where the time goes in v3:
time: 27.1 us; the launch traced here: 27 us
  Pallas kernels  26.3 us (97%)
  between operations  0.64 us (2%)
    pallas_call x1, Pallas kernels, on_device(): pl.pallas_call(functools.partial(kernel, geometry), out_shape=results, in...  25.1 us
    pallas_call x1, Pallas kernels, on_device(): pl.pallas_call(deliver, out_shape=results, in_specs=[vmem] * 3, out_specs...  1.22 us

profile of v3, /device:TPU:0, one launch (start us, length us, event | category | flops | bytes accessed | tf_op | source)
XLA Modules:
  0.0 27.0 jit_solution(14729134174984909116)
XLA Ops:
  0.6 25.1 %shard_map.58 = (f32[32,512]{1,0:T(8,128)S(1)}, f32[32,512]{1,0:T(8,128)S(1)}, bf16[1600,512]{1,0:T(8,128)(2,1)S(1)}) custom-call(bf16[8,5,40,512]{3,2,1,0:T(8,128)(2,1)} %grid4.1, bf16[1600,512]{1,0:T(8,128)(2,1)} %bitcast.3, f32[5,8,40]{2,1,0:T(8,128)} %bitcast.4, bf16[32,512]{1,0:T(8,128)(2,1)} %eig.1), custom_call_target="tpu_custom_call" | custom-call | tf_op jit(solution)/shard_map/pallas_call | solution.py:628
  25.8 1.2 %shard_map.59 = (f32[32,512]{1,0:T(8,128)}, f32[32,512]{1,0:T(8,128)}, bf16[1600,512]{1,0:T(8,128)(2,1)}) custom-call(f32[32,512]{1,0:T(8,128)S(1)} %get-tuple-element.9.corr, f32[32,512]{1,0:T(8,128)S(1)} %get-tuple-element.10.ham, bf16[1600,512]{1,0:T(8,128)(2,1)S(1)} %get-tuple-element.11.rot), custom_call_target="tpu_custom_call" | custom-call | tf_op jit(solution)/shard_map/pallas_call | solution.py:652

commit v4 on v3

--- a/solution.py
+++ b/solution.py
@@ -97,9 +97,9 @@
 
 
 class Stream:
-    def __init__(self, context, source, final, first, last, order, buffers):
+    def __init__(self, context, source, final, both, first, last, order, buffers):
         self.context, self.source, self.final, self.order = context, source, final, order
-        self.rows, self.buffers = slice(first, last), buffers
+        self.rows, self.buffers, self.both = slice(first, last), buffers, both
         self.left, self.phase = list(range(len(context.sizes))), 0
 
     def index(self, values):
@@ -120,6 +120,14 @@
         shape = (self.rows.stop - self.rows.start, ctx.half)
         row = lax.broadcasted_iota(jnp.int32, shape, 0) + (block * ctx.rows + self.rows.start)
         return row == lax.broadcasted_iota(jnp.int32, shape, 1) + parity * ctx.half
+
+    def place(self, values):
+        group = self.order[self.phase]
+        line = 0
+        for d in self.left:
+            if d not in group and d in values:
+                line = line * self.context.sizes[d] + values[d]
+        return tuple(values[d] for d in self.left if d in group), slice(line, line + 1)
 
     def round(self, fixed):
         out, extra = self.buffers[self.phase][:2]
@@ -129,21 +137,22 @@
             short = value.astype(BF16)
             out[at] = short
             rest = jnp.where(self.diagonal(values, self.context.parity), value - short.astype(F32), 0.0)
-            extra[at] = jnp.sum(rest, axis=0, keepdims=True)
+            spot, line = self.place(values)
+            extra[spot + (line,)] = jnp.sum(rest, axis=0, keepdims=True)
 
     def open(self):
         landing, extras = self.buffers[self.phase][2:4]
         self.flights = self.context.copies.group(landing), self.context.copies.group(extras, 1)
 
-    def ship(self, at, slot, device):
+    def ship(self, values, slot, device):
         out, extra, landing, extras = self.buffers[self.phase][:4]
-        self.flights[0].start(out.at[at], landing.at[slot], device)
-        self.flights[1].start(extra.at[at], extras.at[slot], device)
+        self.flights[0].start(out.at[self.index(values)], landing.at[slot], device)
+        self.flights[1].start(extra.at[self.place(values)[0]], extras.at[slot], device)
 
     def send(self, k):
         target, values = self.peers()[k]
         self.round(values)
-        self.ship(self.index(values), k - 1, (self.context.gx, target))
+        self.ship(values, k - 1, (self.context.gx, target))
 
     def start(self):
         self.open()
@@ -155,10 +164,9 @@
         self.round({})
         peers = self.peers()
         for k, (target, values) in enumerate(peers):
-            at = self.index(values)
             if k:
-                self.ship(at, k - 1, (self.context.gx, target))
-            self.ship(at, len(peers) - 1 + k, (self.context.partner, target))
+                self.ship(values, k - 1, (self.context.gx, target))
+            self.ship(values, len(peers) - 1 + k, (self.context.partner, target))
 
     def land(self):
         for flight in self.flights:
@@ -169,7 +177,8 @@
         out, extra, landing, extras = self.buffers[self.phase][:4]
         many = len(self.peers())
         at = self.index(self.peers()[0][1])
-        mine = [(out[at], extra[at])] + [(landing[k], extras[k]) for k in range(many - 1)]
+        own = extra[self.place(self.peers()[0][1])[0]]
+        mine = [(out[at], own)] + [(landing[k], extras[k]) for k in range(many - 1)]
         across = [(landing[k], extras[k]) for k in range(many - 1, 2 * many - 1)]
         parity = self.context.parity
         for column, side, parts in zip(columns, (parity, 1 - parity), (mine, across)):
@@ -190,7 +199,7 @@
             rest = 0.0
             for k in range(landing.shape[0]):
                 total = total + landing[(k,) + keep].astype(F32)
-                rest = rest + extras[(k,) + keep]
+                rest = rest + extras[k, self.place(values)[1]]
             result[keep + (Ellipsis,)] = total + jnp.where(self.diagonal(values, self.context.parity), rest, 0.0)
         self.source = result
         self.left = [d for d in self.left if d not in own]
@@ -299,9 +308,13 @@
             elif at == 1:
                 state[1] = coef_send(coef_plan[-2], held)
             elif at == 2:
+                y, x = coef_plan[-1][0], coef_plan[-2][0]
                 coef_wait(state[1])
-                d, = coef_plan[-2]
-                state[3] += coef_send(coef_plan[-1], held[:d] + (1 - digits[d],) + held[d + 1:])
+                across = held[:x] + (1 - digits[x],) + held[x + 1:]
+                relayed_y = coef_send((y,), (0,) + across[1:])
+                coef_wait(state[3])
+                across = held[:y] + (1 - digits[y],) + held[y + 1:]
+                state[3] = relayed_y + coef_send((x,), (1,) + across[1:])
             else:
                 coef_wait(state[3])
                 coef_exchange()
@@ -398,11 +411,11 @@
 
     scale = 1.0 / (cells * gyz_size)
 
-    def streams(plan, source, final):
-        return [Stream(context, source, final, first, last, order, [[next(taken) for _ in range(5)] for _ in order])
+    def streams(plan, source, final, both):
+        return [Stream(context, source, final, both, first, last, order, [[next(taken) for _ in range(5)] for _ in order])
                 for first, last, order in plan]
 
-    ham_streams, corr_streams = streams(ham_plan, sum_h, ham_out), streams(corr_plan, sum_c, corr_out)
+    ham_streams, corr_streams = streams(ham_plan, sum_h, ham_out, direct), streams(corr_plan, sum_c, corr_out, False)
 
     def begin(group):
         for stream in group:
@@ -412,11 +425,11 @@
         for stream in group:
             if stream.phase == len(stream.order):
                 continue
-            if direct and stream.phase == len(stream.order) - 1:
+            if stream.both and stream.phase == len(stream.order) - 1:
                 stream.finish_both((mine, other), scale)
                 continue
             stream.finish()
-            if direct and stream.phase == len(stream.order) - 1:
+            if stream.both and stream.phase == len(stream.order) - 1:
                 stream.start_both()
             elif stream.phase < len(stream.order):
                 stream.start()
@@ -533,7 +546,7 @@
 
     last = []
     if relayed:
-        steps = ["corr", "coef", "ham", "coef", "rot", "corr", "ham"]
+        steps = ["coef", "corr", "ham", "coef", "corr", "rot", "ham"]
     else:
         steps = ["coef"] * (coef_steps - coef_state[0]) + ["rot"]
         steps += ["corr"] * len(corr_plan[0][2]) + ["ham"] * len(ham_plan[0][2])
@@ -541,7 +554,7 @@
         if step == "corr":
             corr_step()
             if corr_streams[0].phase == len(corr_streams[0].order):
-                last += [] if direct else [last_sum(corr_streams, gx_c, corr_out)]
+                last += [last_sum(corr_streams, gx_c, corr_out)]
         if step == "ham":
             at = ham_streams[0].phase
             for which, stream in enumerate(ham_streams):
@@ -601,22 +614,22 @@
     ham_plan, corr_plan, coef_plan = plans_of(rows, sizes)
     copy_count = 4 + peer_count(sizes, ham_plan[0][2][0]) + len(ham_plan) - 1
     copy_count += sum(2 * len(order) for _, _, order in ham_plan + corr_plan)
-    copy_count += len(coef_plan) + (sizes == (2, 2, 2, 2)) - 1
-    copy_count += 0 if gx_size == 2 else 2 * (gx_size // 2)
+    copy_count += len(coef_plan) + 2 * (sizes == (2, 2, 2, 2)) - 1
+    copy_count += 1 if gx_size == 2 else 2 * (gx_size // 2)
     geometry = (gx_size, gyz_size, cx, cy, cz, width, rows, sizes, copy_count)
 
     buffers = []
-    for first, last, order in ham_plan + corr_plan:
+    for at, (first, last, order) in enumerate(ham_plan + corr_plan):
         left = list(range(count))
         for group in order:
             many = peer_count(sizes, group)
-            many = 2 * many - 1 if gx_size == 2 and group == order[-1] else many - 1
-            whole = tuple(sizes[i] for i in left)
+            many = 2 * many - 1 if gx_size == 2 and at < len(ham_plan) and group == order[-1] else many - 1
+            whole, spots = tuple(sizes[i] for i in left), tuple(sizes[i] for i in left if i in group)
             left = [d for d in left if d not in group]
             kept = tuple(sizes[i] for i in left)
-            cut, line = (last - first, half), (1, half)
-            buffers += [pltpu.VMEM(whole + cut, BF16), pltpu.VMEM(whole + line, F32),
-                        pltpu.VMEM((many,) + kept + cut, BF16), pltpu.VMEM((many,) + kept + line, F32),
+            cut, lines = (last - first, half), (math.prod(kept), half)
+            buffers += [pltpu.VMEM(whole + cut, BF16), pltpu.VMEM(spots + lines, F32),
+                        pltpu.VMEM((many,) + kept + cut, BF16), pltpu.VMEM((many,) + lines, F32),
                         pltpu.VMEM(kept + cut, F32)]
 
     cut_x = (cx + 1) // 2

time: 27.1 us -> 27.1 us (level)
  no operation moved by 1% of the time
where the time goes in v4:
time: 27.1 us; the launch traced here: 26.9 us
  Pallas kernels  26.3 us (97%)
  between operations  0.64 us (2%)
    pallas_call x1, Pallas kernels, on_device(): pl.pallas_call(functools.partial(kernel, geometry), out_shape=results, in...  25.1 us
    pallas_call x1, Pallas kernels, on_device(): pl.pallas_call(deliver, out_shape=results, in_specs=[vmem] * 3, out_specs...  1.22 us

profile of v4, /device:TPU:0, one launch (start us, length us, event | category | flops | bytes accessed | tf_op | source)
XLA Modules:
  0.0 26.9 jit_solution(14913903965296772621)
XLA Ops:
  0.6 25.1 %shard_map.58 = (f32[32,512]{1,0:T(8,128)S(1)}, f32[32,512]{1,0:T(8,128)S(1)}, bf16[1600,512]{1,0:T(8,128)(2,1)S(1)}) custom-call(bf16[8,5,40,512]{3,2,1,0:T(8,128)(2,1)} %grid4.1, bf16[1600,512]{1,0:T(8,128)(2,1)} %bitcast.3, f32[5,8,40]{2,1,0:T(8,128)} %bitcast.4, bf16[32,512]{1,0:T(8,128)(2,1)} %eig.1), custom_call_target="tpu_custom_call" | custom-call | tf_op jit(solution)/shard_map/pallas_call | solution.py:641
  25.7 1.2 %shard_map.59 = (f32[32,512]{1,0:T(8,128)}, f32[32,512]{1,0:T(8,128)}, bf16[1600,512]{1,0:T(8,128)(2,1)}) custom-call(f32[32,512]{1,0:T(8,128)S(1)} %get-tuple-element.9.corr, f32[32,512]{1,0:T(8,128)S(1)} %get-tuple-element.10.ham, bf16[1600,512]{1,0:T(8,128)(2,1)S(1)} %get-tuple-element.11.rot), custom_call_target="tpu_custom_call" | custom-call | tf_op jit(solution)/shard_map/pallas_call | solution.py:665

commit v5 on v4

--- a/solution.py
+++ b/solution.py
@@ -33,13 +33,13 @@
 
 
 class Group:
-    def __init__(self, copies, send_sem, recv_sem, whole):
-        self.copies, self.send_sem, self.recv_sem, self.whole = copies, send_sem, recv_sem, whole
-
-    def start(self, src, dst, device_id):
-        self.copies.sent[self.send_sem] += bytes_of(src)
+    def __init__(self, copies, recv_sem, whole):
+        self.copies, self.recv_sem, self.whole = copies, recv_sem, whole
+
+    def start(self, src, dst, device_id, kind=0):
+        self.copies.sent[kind] += bytes_of(src)
         pltpu.make_async_remote_copy(
-            src_ref=src, dst_ref=dst, send_sem=self.copies.send_sems.at[self.send_sem],
+            src_ref=src, dst_ref=dst, send_sem=self.copies.send_sems.at[kind],
             recv_sem=self.recv_sem, device_id=device_id, device_id_type=MESH).start()
 
     def wait_recv(self):
@@ -51,9 +51,9 @@
         self.send_sems, self.recv_sems, self.measures = send_sems, recv_sems, measures
         self.used, self.sent = 0, [0, 0]
 
-    def group(self, whole, kind=0):
+    def group(self, whole):
         self.used += 1
-        return Group(self, kind, self.recv_sems.at[self.used - 1], whole)
+        return Group(self, self.recv_sems.at[self.used - 1], whole)
 
     def span(self, size, kind=0):
         measure = self.measures[kind]
@@ -94,6 +94,11 @@
 
 def copies_of(sizes, order):
     return sum(peer_count(sizes, group) - 1 for group in order)
+
+
+def far_first(group, many):
+    order = {Z: [2, 1, 3], XY: [3, 1, 2]}.get(group)
+    return order if order and many == 4 else list(range(1, many))
 
 
 class Stream:
@@ -142,12 +147,12 @@
 
     def open(self):
         landing, extras = self.buffers[self.phase][2:4]
-        self.flights = self.context.copies.group(landing), self.context.copies.group(extras, 1)
+        self.flight = self.context.copies.group(self.context.copies.span(bytes_of(landing) + bytes_of(extras), 1))
 
     def ship(self, values, slot, device):
         out, extra, landing, extras = self.buffers[self.phase][:4]
-        self.flights[0].start(out.at[self.index(values)], landing.at[slot], device)
-        self.flights[1].start(extra.at[self.place(values)[0]], extras.at[slot], device)
+        self.flight.start(out.at[self.index(values)], landing.at[slot], device)
+        self.flight.start(extra.at[self.place(values)[0]], extras.at[slot], device, 1)
 
     def send(self, k):
         target, values = self.peers()[k]
@@ -156,21 +161,21 @@
 
     def start(self):
         self.open()
-        for k in range(1, len(self.peers())):
+        for k in far_first(self.order[self.phase], len(self.peers())):
             self.send(k)
 
     def start_both(self):
         self.open()
         self.round({})
         peers = self.peers()
-        for k, (target, values) in enumerate(peers):
+        for k in far_first(self.order[self.phase], len(peers)) + [0]:
+            target, values = peers[k]
             if k:
                 self.ship(values, k - 1, (self.context.gx, target))
             self.ship(values, len(peers) - 1 + k, (self.context.partner, target))
 
     def land(self):
-        for flight in self.flights:
-            flight.wait_recv()
+        self.flight.wait_recv()
 
     def finish_both(self, columns, scale):
         self.land()
@@ -505,7 +510,7 @@
     for j in range(bands // rows):
         late[block_index(j)] = (-0.5 * value[j * rows:(j + 1) * rows]).astype(BF16)
     pieces = [(ham_streams[0], k, at) for k, at in enumerate(ham_streams[0].index(values) for _, values in ham_streams[0].peers())]
-    pieces = pieces[1:] + [(stream, None, everything[:-1]) for stream in ham_streams[1:]] + pieces[:1]
+    pieces = [(stream, None, everything[:-1]) for stream in ham_streams[1:]] + [pieces[k] for k in far_first(ham_streams[0].order[0], len(pieces))] + pieces[:1]
     pair_copies_h = []
     for stream, k, at in pieces:
         at = at + (stream.rows,)
@@ -613,7 +618,7 @@
     flat = bands.reshape(cells, width)
     ham_plan, corr_plan, coef_plan = plans_of(rows, sizes)
     copy_count = 4 + peer_count(sizes, ham_plan[0][2][0]) + len(ham_plan) - 1
-    copy_count += sum(2 * len(order) for _, _, order in ham_plan + corr_plan)
+    copy_count += sum(len(order) for _, _, order in ham_plan + corr_plan)
     copy_count += len(coef_plan) + 2 * (sizes == (2, 2, 2, 2)) - 1
     copy_count += 1 if gx_size == 2 else 2 * (gx_size // 2)
     geometry = (gx_size, gyz_size, cx, cy, cz, width, rows, sizes, copy_count)

time: 27.1 us -> 26.7 us (0.985)
  Pallas kernels: 26.3 us -> 25.9 us
    pallas_call x1, Pallas kernels: 25.1 us -> 24.7 us  [on_device(): pl.pallas_call(functools.partial(kernel, geometry), out_shape=results, in...]
where the time goes in v5:
time: 26.7 us; the launch traced here: 26.6 us
  Pallas kernels  25.9 us (97%)
  between operations  0.64 us (2%)
    pallas_call x1, Pallas kernels, on_device(): pl.pallas_call(functools.partial(kernel, geometry), out_shape=results, in...  24.7 us
    pallas_call x1, Pallas kernels, on_device(): pl.pallas_call(deliver, out_shape=results, in_specs=[vmem] * 3, out_specs...  1.22 us

profile of v5, /device:TPU:0, one launch (start us, length us, event | category | flops | bytes accessed | tf_op | source)
XLA Modules:
  0.0 26.6 jit_solution(9751322468374179247)
XLA Ops:
  0.6 24.7 %shard_map.58 = (f32[32,512]{1,0:T(8,128)S(1)}, f32[32,512]{1,0:T(8,128)S(1)}, bf16[1600,512]{1,0:T(8,128)(2,1)S(1)}) custom-call(bf16[8,5,40,512]{3,2,1,0:T(8,128)(2,1)} %grid4.1, bf16[1600,512]{1,0:T(8,128)(2,1)} %bitcast.3, f32[5,8,40]{2,1,0:T(8,128)} %bitcast.4, bf16[32,512]{1,0:T(8,128)(2,1)} %eig.1), custom_call_target="tpu_custom_call" | custom-call | tf_op jit(solution)/shard_map/pallas_call | solution.py:646
  25.3 1.2 %shard_map.59 = (f32[32,512]{1,0:T(8,128)}, f32[32,512]{1,0:T(8,128)}, bf16[1600,512]{1,0:T(8,128)(2,1)}) custom-call(f32[32,512]{1,0:T(8,128)S(1)} %get-tuple-element.9.corr, f32[32,512]{1,0:T(8,128)S(1)} %get-tuple-element.10.ham, bf16[1600,512]{1,0:T(8,128)(2,1)S(1)} %get-tuple-element.11.rot), custom_call_target="tpu_custom_call" | custom-call | tf_op jit(solution)/shard_map/pallas_call | solution.py:670

commit v6 on v5

--- a/solution.py
+++ b/solution.py
@@ -519,10 +519,11 @@
     with scope('pair_h'):
         ham_streams[0].open()
         pair_copy_h.wait_recv()
+        sum_h[...] = ham[everything + (mine,)] + pair_h[...]
         for (stream, k, at), copy in zip(pieces, pair_copies_h):
             at = at + (stream.rows,)
             copy.wait_recv()
-            sum_h[at] = ham[at + (mine,)] + pair_h[at] + pair_l[at].astype(F32)
+            sum_h[at] = sum_h[at] + pair_l[at].astype(F32)
             if k is None:
                 stream.start()
             elif k:

time: 26.7 us -> 26.8 us (level)
  no operation moved by 1% of the time
where the time goes in v6:
time: 26.8 us; the launch traced here: 26.7 us
  Pallas kernels  26 us (97%)
  between operations  0.64 us (2%)
    pallas_call x1, Pallas kernels, on_device(): pl.pallas_call(functools.partial(kernel, geometry), out_shape=results, in...  24.8 us
    pallas_call x1, Pallas kernels, on_device(): pl.pallas_call(deliver, out_shape=results, in_specs=[vmem] * 3, out_specs...  1.22 us

profile of v6, /device:TPU:0, one launch (start us, length us, event | category | flops | bytes accessed | tf_op | source)
XLA Modules:
  0.0 26.7 jit_solution(3490389660544077351)
XLA Ops:
  0.6 24.8 %shard_map.58 = (f32[32,512]{1,0:T(8,128)S(1)}, f32[32,512]{1,0:T(8,128)S(1)}, bf16[1600,512]{1,0:T(8,128)(2,1)S(1)}) custom-call(bf16[8,5,40,512]{3,2,1,0:T(8,128)(2,1)} %grid4.1, bf16[1600,512]{1,0:T(8,128)(2,1)} %bitcast.3, f32[5,8,40]{2,1,0:T(8,128)} %bitcast.4, bf16[32,512]{1,0:T(8,128)(2,1)} %eig.1), custom_call_target="tpu_custom_call" | custom-call | tf_op jit(solution)/shard_map/pallas_call | solution.py:647
  25.4 1.2 %shard_map.59 = (f32[32,512]{1,0:T(8,128)}, f32[32,512]{1,0:T(8,128)}, bf16[1600,512]{1,0:T(8,128)(2,1)}) custom-call(f32[32,512]{1,0:T(8,128)S(1)} %get-tuple-element.9.corr, f32[32,512]{1,0:T(8,128)S(1)} %get-tuple-element.10.ham, bf16[1600,512]{1,0:T(8,128)(2,1)S(1)} %get-tuple-element.11.rot), custom_call_target="tpu_custom_call" | custom-call | tf_op jit(solution)/shard_map/pallas_call | solution.py:671

commit v7 on v5

--- a/solution.py
+++ b/solution.py
@@ -96,8 +96,8 @@
     return sum(peer_count(sizes, group) - 1 for group in order)
 
 
-def far_first(group, many):
-    order = {Z: [2, 1, 3], XY: [3, 1, 2]}.get(group)
+def far_first(group, many, last=False):
+    order = ({Z: [3, 2, 1], XY: [3, 1, 2]} if last else {Z: [2, 1, 3], XY: [3, 1, 2]}).get(group)
     return order if order and many == 4 else list(range(1, many))
 
 
@@ -168,7 +168,7 @@
         self.open()
         self.round({})
         peers = self.peers()
-        for k in far_first(self.order[self.phase], len(peers)) + [0]:
+        for k in far_first(self.order[self.phase], len(peers), True) + [0]:
             target, values = peers[k]
             if k:
                 self.ship(values, k - 1, (self.context.gx, target))

time: 26.7 us -> 26.7 us (level)
  no operation moved by 1% of the time
where the time goes in v7:
time: 26.7 us; the launch traced here: 26.6 us
  Pallas kernels  25.9 us (97%)
  between operations  0.64 us (2%)
    pallas_call x1, Pallas kernels, on_device(): pl.pallas_call(functools.partial(kernel, geometry), out_shape=results, in...  24.7 us
    pallas_call x1, Pallas kernels, on_device(): pl.pallas_call(deliver, out_shape=results, in_specs=[vmem] * 3, out_specs...  1.22 us

profile of v7, /device:TPU:0, one launch (start us, length us, event | category | flops | bytes accessed | tf_op | source)
XLA Modules:
  0.0 26.6 jit_solution(2736002411381991957)
XLA Ops:
  0.6 24.7 %shard_map.58 = (f32[32,512]{1,0:T(8,128)S(1)}, f32[32,512]{1,0:T(8,128)S(1)}, bf16[1600,512]{1,0:T(8,128)(2,1)S(1)}) custom-call(bf16[8,5,40,512]{3,2,1,0:T(8,128)(2,1)} %grid4.1, bf16[1600,512]{1,0:T(8,128)(2,1)} %bitcast.3, f32[5,8,40]{2,1,0:T(8,128)} %bitcast.4, bf16[32,512]{1,0:T(8,128)(2,1)} %eig.1), custom_call_target="tpu_custom_call" | custom-call | tf_op jit(solution)/shard_map/pallas_call | solution.py:646
  25.3 1.2 %shard_map.59 = (f32[32,512]{1,0:T(8,128)}, f32[32,512]{1,0:T(8,128)}, bf16[1600,512]{1,0:T(8,128)(2,1)}) custom-call(f32[32,512]{1,0:T(8,128)S(1)} %get-tuple-element.9.corr, f32[32,512]{1,0:T(8,128)S(1)} %get-tuple-element.10.ham, bf16[1600,512]{1,0:T(8,128)(2,1)S(1)} %get-tuple-element.11.rot), custom_call_target="tpu_custom_call" | custom-call | tf_op jit(solution)/shard_map/pallas_call | solution.py:670
